TPU v7x, 256 devices: a whole 4x4x8 slice. The times are simulated.
256 devices in a mesh: win: 128 (over y, x, z), head: 2 (over core).
Axes of the slice: x: 4, y: 4, z: 8, core: 2. Of those that a mesh axis runs over, the one named last changes fastest.
Arguments:
- coords: float32 [3, 4096, 128], P(None, 'win', 'head'), may hold values from -8 to 16
- noise: float32 [3, 4096, 128], P(None, 'win', 'head'), may hold values from -6 to 6
- sigma: float32 [1], replicated, may hold values from 0.25 to 1
- atom_single: bfloat16 [4096, 128, 128], P('win', 'head'), may hold values from -6 to 6
- token_single: bfloat16 [65536, 384], P('win'), may hold values from -6 to 6
- atom_token: int32 [4096, 128], P('win', 'head'), may hold values from 0 to 15, never falling along the last dimension, each value on 1 to 64 neighbouring positions
- window_count: int32 [128], replicated, may hold values from 1 to 31, as said below
- pair_bias: bfloat16 [4, 4096, 128, 128], P('head', 'win'), may hold values from -6 to 260
- token_weight: bfloat16 [384, 128], replicated, may hold values from -0.3125 to 0.3125
- cond_gain: float32 [128], replicated, may hold values from 0.25 to 1.75
- position_weight: float32 [3, 128], replicated, may hold values from -3.5 to 3.5
- ada_weight: bfloat16 [3, 6, 128, 128], replicated, may hold values from -0.5 to 0.5
- ada_bias: float32 [3, 6, 128], replicated, may hold values from -4 to 4
- attn_weight: bfloat16 [3, 4, 128, 128], P(None, None, None, 'head'), may hold values from -0.5 to 0.5
- out_weight: bfloat16 [3, 128, 128], P(None, 'head'), may hold values from -0.5 to 0.5
- gateup_weight: bfloat16 [3, 2, 128, 256], replicated, may hold values from -0.5 to 0.5
- down_weight: bfloat16 [3, 256, 128], replicated, may hold values from -0.375 to 0.375
- final_weight: bfloat16 [3, 128], replicated, may hold values from -0.5 to 0.5
Outputs:
- denoised: float32 [3, 4096, 128], P(None, 'win', 'head')
Inputs may be any that keep to these rules, and one draw needn't show every extreme that they name: window_count[d] + window_count[d + 64] <= 32 for every d < 64, with equality for some d.
All inputs are finite; a program needn't handle non-finite values.
Results may differ from a plain program's by a relative error of at most 0.005.
Values may be sent and summed in bfloat16 or wider, within the bound.
A program may use at most 128 MiB of HBM per device.

v0:
```python
import jax
import jax.numpy as jnp
from jax import lax
from jax.sharding import Mesh
from jax.sharding import PartitionSpec as P

HEAD_DIM = 32
QW = 128
TOKW = 16
BLOCKS = 3
WIN = ("win_0", "win_1", "win_2")
WIN_HEAD = ("win_0", "win_1", "win_2", "head")


EPSILON = 1e-05


def rows_first(arrays, axis, dims):
    turned = [jnp.moveaxis(a, dim, 0) for a, dim in zip(arrays, dims)]
    widths = [t[0].size for t in turned]
    both = jnp.concatenate([t.reshape(-1, w) for t, w in zip(turned, widths)], axis=1)
    filled = lax.all_gather(both, axis, axis=0, tiled=True)
    parts = jnp.split(filled, [sum(widths[:k]) for k in range(1, len(widths))], axis=1)
    return tuple(
        (
            jnp.moveaxis(b.reshape(-1, *t.shape[1:]), 0, dim)
            for b, t, dim in zip(parts, turned, dims)
        )
    )


def in_one_piece(arrays, axis, split_dim, concat_dim, along):
    ends, at = ([], 0)
    for a in arrays[:-1]:
        at += a.shape[along]
        ends.append(at)
    both = jnp.concatenate(arrays, axis=along)
    return tuple(
        jnp.split(
            lax.all_to_all(both, axis, split_axis=split_dim, concat_axis=concat_dim, tiled=True),
            ends,
            axis=along,
        )
    )


def by_axis(array, axes):
    for axis in axes:
        array = lax.psum(array, axis)
    return array


def layer_norm(values):
    average = jnp.mean(values, axis=-1, keepdims=True)
    centred = values - average
    variance = jnp.mean(centred * centred, axis=-1, keepdims=True)
    return centred * lax.rsqrt(variance + EPSILON)


def lookup_tokens(tokens_here, local_token):
    token_grid = tokens_here.reshape(local_token.shape[0], TOKW, -1)
    one_hot = (local_token[:, :, None] == jnp.arange(TOKW, dtype=jnp.int32)).astype(jnp.bfloat16)
    return jnp.einsum(
        "wqt,wtc->wqc", one_hot, token_grid, preferred_element_type=jnp.float32
    ).astype(jnp.bfloat16)


def project_rows(weight_set, portion):
    return jnp.einsum(
        "wqc,jcd->jwqd", portion, weight_set, preferred_element_type=jnp.float32
    ).astype(jnp.bfloat16)


def window_net(single, looked, scaled, pair_terms, weights_all, project_fn, output_fn):
    cond_gain, position_weight, ada_weight, ada_bias, gateup_weight, down_weight, final_weight = (
        weights_all
    )
    condition = single.astype(jnp.float32) + looked.astype(jnp.float32)
    cond_norm = (layer_norm(condition) * cond_gain).astype(jnp.bfloat16)
    stream = condition + jnp.einsum(
        "kwq,kc->wqc", scaled, position_weight, precision=lax.Precision.HIGHEST
    )
    window_total = single.shape[0]
    for block_index in range(BLOCKS):
        ada_terms = (
            jnp.einsum(
                "wqc,jcd->jwqd",
                cond_norm,
                ada_weight[block_index],
                preferred_element_type=jnp.float32,
            )
            + ada_bias[block_index][:, None, None, :]
        )
        normed = (layer_norm(stream) * jax.nn.sigmoid(ada_terms[0]) + ada_terms[1]).astype(
            jnp.bfloat16
        )
        projected = project_fn(block_index, normed)
        row_count = projected.shape[2]
        query_rows = projected[0].reshape(window_total, row_count, -1, HEAD_DIM)
        key_rows = projected[1].reshape(window_total, row_count, -1, HEAD_DIM)
        value_rows = projected[2].reshape(window_total, row_count, -1, HEAD_DIM)
        gate_logits = (
            projected[3].reshape(window_total, row_count, -1, HEAD_DIM).astype(jnp.float32)
        )
        scores = jnp.einsum(
            "wqhd,wkhd->hwqk", query_rows, key_rows, preferred_element_type=jnp.float32
        )
        scores = scores * HEAD_DIM ** (-0.5) + pair_terms.astype(jnp.float32)
        row_max = jnp.max(scores, axis=-1, keepdims=True)
        exponent = jnp.exp(scores - row_max)
        weights = (exponent / jnp.sum(exponent, axis=-1, keepdims=True)).astype(jnp.bfloat16)
        attended = jnp.einsum(
            "hwqk,wkhd->wqhd", weights, value_rows, preferred_element_type=jnp.float32
        )
        attended = (
            (attended * jax.nn.sigmoid(gate_logits))
            .astype(jnp.bfloat16)
            .reshape(window_total, row_count, -1)
        )
        update = output_fn(block_index, attended)
        stream = stream + jax.nn.sigmoid(ada_terms[2]) * update
        normed_two = (layer_norm(stream) * jax.nn.sigmoid(ada_terms[3]) + ada_terms[4]).astype(
            jnp.bfloat16
        )
        gate_part = jnp.einsum(
            "wqc,ch->wqh",
            normed_two,
            gateup_weight[block_index, 0],
            preferred_element_type=jnp.float32,
        )
        up_part = jnp.einsum(
            "wqc,ch->wqh",
            normed_two,
            gateup_weight[block_index, 1],
            preferred_element_type=jnp.float32,
        )
        hidden = (jax.nn.silu(gate_part) * up_part).astype(jnp.bfloat16)
        down_part = jnp.einsum(
            "wqh,hc->wqc", hidden, down_weight[block_index], preferred_element_type=jnp.float32
        )
        stream = stream + jax.nn.sigmoid(ada_terms[5]) * down_part
    final_norm = layer_norm(stream).astype(jnp.bfloat16)
    return jnp.einsum("wqc,kc->kwq", final_norm, final_weight, preferred_element_type=jnp.float32)


def run_net(single, looked, scaled, pair_terms, weights_all, attn_weight, out_weight):
    attn_full, out_full = rows_first((attn_weight, out_weight), "head", (3, 1))
    single_own, looked_own = in_one_piece((single, looked), "head", 0, 1, 2)
    terms_own = lax.all_to_all(pair_terms, "head", split_axis=1, concat_axis=0, tiled=True)
    scaled_own = lax.all_to_all(scaled, "head", split_axis=1, concat_axis=2, tiled=True)

    def project_local(block_index, normed):
        return project_rows(attn_full[block_index], normed)

    def output_local(block_index, attended):
        return jnp.einsum(
            "wqd,dc->wqc", attended, out_full[block_index], preferred_element_type=jnp.float32
        )

    update_own = window_net(
        single_own, looked_own, scaled_own, terms_own, weights_all, project_local, output_local
    )
    return lax.all_to_all(update_own, "head", split_axis=2, concat_axis=1, tiled=True)


def local(
    coords,
    noise,
    sigma,
    atom_single,
    token_single,
    atom_token,
    window_count,
    pair_bias,
    token_weight,
    cond_gain,
    position_weight,
    ada_weight,
    ada_bias,
    attn_weight,
    out_weight,
    gateup_weight,
    down_weight,
    final_weight,
):
    sigma_value = sigma[0]
    noisy_pos = coords + sigma_value * noise
    slot_total = atom_single.shape[0]
    device_id = lax.axis_index(WIN)
    own_count = window_count[device_id]
    slot_ids = jnp.arange(slot_total, dtype=jnp.int32)
    live_mask = (slot_ids < own_count).astype(jnp.float32)
    partial_pos = jnp.sum(noisy_pos * live_mask[None, :, None], axis=(1, 2))
    totals = by_axis(partial_pos, WIN_HEAD)
    centre = totals / (QW * jnp.sum(window_count).astype(jnp.float32))
    shifted = noisy_pos - centre[:, None, None]
    inverse = 1.0 / (1.0 + sigma_value * sigma_value)
    scaled = shifted * jnp.sqrt(inverse)
    token_proj = jnp.dot(token_single, token_weight, preferred_element_type=jnp.float32).astype(
        jnp.bfloat16
    )
    looked = lookup_tokens(token_proj, atom_token)
    weights_all = (
        cond_gain,
        position_weight,
        ada_weight,
        ada_bias,
        gateup_weight,
        down_weight,
        final_weight,
    )
    update_pos = run_net(
        atom_single, looked, scaled, pair_bias, weights_all, attn_weight, out_weight
    )
    denoised = shifted * inverse + sigma_value * jnp.sqrt(inverse) * update_pos
    return denoised * live_mask[None, :, None]


def solution(mesh):
    torus = Mesh(
        mesh.devices.reshape(4, 4, 8, mesh.shape["head"]), ("win_0", "win_1", "win_2", "head")
    )
    in_specs = (
        P(None, WIN, "head"),
        P(None, WIN, "head"),
        P(),
        P(WIN, "head", None),
        P(WIN, None),
        P(WIN, "head"),
        P(),
        P("head", WIN, None, None),
        P(),
        P(),
        P(),
        P(),
        P(),
        P(None, None, None, "head"),
        P(None, "head", None),
        P(),
        P(),
        P(),
    )
    out_specs = P(None, WIN, "head")
    return jax.shard_map(local, mesh=torus, in_specs=in_specs, out_specs=out_specs, check_vma=False)
```

profile of v0, /device:TPU:1, one launch (start us, length us, event | category | flops | bytes accessed | tf_op | source)
XLA Modules:
  0.0 160.6 jit_solution(1262722235757631288)
XLA Ops:
  0.0 1.4 dynamic_slice.3
  2.7 1.0 multiply_reduce_fusion.8
  3.7 9.5 %psum.28 = f32[3]{0:T(128)S(1)} all-reduce(f32[3]{0:T(128)S(1)} %get-tuple-element.5), channel_id=1, replica_groups=mesh['win_0'=4,'win_1'=4,'win_2'=8,'head'=2] {'win_0'}, use_global_device_ids=true, to_apply=%region_1.0 | all-reduce | flops 3 | bytes 24 | tf_op jit(solution)/shard_map/psum | solution.py:49
  13.2 1.3 reduce_sum.190
  14.5 8.7 %psum.29 = f32[3]{0:T(128)S(1)} all-reduce(f32[3]{0:T(128)S(1)} %psum.28), channel_id=1, replica_groups=mesh['win_0'=4,'win_1'=4,'win_2'=8,'head'=2] {'win_1'}, use_global_device_ids=true, to_apply=%region_2.0 | all-reduce | flops 3 | bytes 24 | tf_op jit(solution)/shard_map/psum | solution.py:49
  23.3 16.2 %psum.30 = f32[3]{0:T(128)S(1)} all-reduce(f32[3]{0:T(128)S(1)} %psum.29), channel_id=1, replica_groups=mesh['win_0'=4,'win_1'=4,'win_2'=8,'head'=2] {'win_2'}, use_global_device_ids=true, to_apply=%region_3.0 | all-reduce | flops 3 | bytes 24 | tf_op jit(solution)/shard_map/psum | solution.py:49
  39.6 10.3 %psum.31 = f32[3]{0:T(128)S(1)} all-reduce(f32[3]{0:T(128)S(1)} %psum.30), channel_id=1, replica_groups=mesh['win_0'=4,'win_1'=4,'win_2'=8,'head'=2] {'head'}, use_global_device_ids=true, to_apply=%region_4.0 | all-reduce | flops 3 | bytes 24 | tf_op jit(solution)/shard_map/psum | solution.py:49
  51.4 3.6 %all-to-all-start.1 = ((f32[2,1,3072]{2,1,0:T(1,128)}), f32[2,1,3072]{2,1,0:T(1,128)S(1)}, u32[]{:S(2)}, u32[]{:S(2)}) async-start(f32[2,1,3072]{2,1,0:T(1,128)} %reshape.274), calls=%async_computation.1 | async-start | bytes 49152 | tf_op jit(solution)/shard_map/all_to_all | solution.py:150
  55.0 1.2 convolution_convert_fusion.1
  56.2 1.2 convolution_convert_fusion
  57.4 2.2 %pad_maximum_fusion = bf16[32,64,256]{2,1,0:T(8,128)(2,1)} fusion(bf16[32,64,128]{2,1,0:T(8,128)(2,1)S(1)} %convolution_convert_fusion, bf16[32,64,128]{2,1,0:T(8,128)(2,1)} %param.21), kind=kLoop, calls=%fused_computation.139 | loop fusion | flops 2097152 | bytes 2097152 | tf_op jit(solution)/shard_map/concatenate | solution.py:37
  60.2 3.6 %all-to-all-start = ((bf16[32,64,256]{2,1,0:T(8,128)(2,1)}), bf16[32,64,256]{2,1,0:T(8,128)(2,1)S(1)}, u32[]{:S(2)}, u32[]{:S(2)}) async-start(bf16[32,64,256]{2,1,0:T(8,128)(2,1)} %pad_maximum_fusion), calls=%async_computation | async-start | bytes 2097152 | tf_op jit(solution)/shard_map/all_to_all | solution.py:40
  64.2 1.4 reduce
  65.9 1.5 copy.260
  67.4 3.8 %all-to-all-start.2 = ((bf16[2,32,128,128]{3,2,0,1:T(8,128)(2,1)}), bf16[2,32,128,128]{3,2,0,1:T(8,128)(2,1)S(1)}, u32[]{:S(2)}, u32[]{:S(2)}) async-start(bf16[2,32,128,128]{3,2,0,1:T(8,128)(2,1)} %copy.260), calls=%async_computation.2 | async-start | bytes 4194304 | tf_op jit(solution)/shard_map/all_to_all | solution.py:149
  71.3 1.1 fusion.186
  72.6 1.3 copy.331
  75.0 1.1 fusion.187
  76.1 0.9 copy-done.9
  79.4 1.0 pad_maximum_fusion.1
  80.3 2.3 %all_gather.3 = bf16[128,1920]{1,0:T(8,128)(2,1)S(1)} all-gather(bf16[64,1920]{1,0:T(8,128)(2,1)S(1)} %pad_maximum_fusion.1), channel_id=1, replica_groups=mesh['win_0'=4,'win_1'=4,'win_2'=8,'head'=2] {'head'}, dimensions={0}, use_global_device_ids=true | all-gather | bytes 737280 | tf_op jit(solution)/shard_map/all_gather | solution.py:22
  83.5 0.8 split.19
  84.3 1.2 copy.255
  85.5 0.9 copy.256
  86.5 1.1 fusion.118
  88.4 2.0 %add_bitcast_fusion.2 = f32[6,16,128,128]{2,3,1,0:T(8,128)S(1)} fusion(f32[6,128]{1,0:T(8,128)S(1)} %get-tuple-element.19, bf16[16,128,128,1]{1,2,0,3:T(8,128)(2,1)S(1)} %fusion.118, bf16[3,6,128,128]{3,2,1,0:T(8,128)(2,1)} %param.29), kind=kOutput, calls=%fused_computation.5 | convolution fusion | flops 404226048 | bytes 7015424 | tf_op jit(solution)/shard_map/wqc,jcd->jwqd/dot_general | solution.py:86
  90.4 1.8 %convert_bitcast_fusion.2 = bf16[4,16,128,128]{2,3,1,0:T(8,128)(2,1)S(1)} fusion(f32[6,16,128,128]{2,3,1,0:T(8,128)S(1)} %add_bitcast_fusion.2, f32[16,128,128]{1,2,0:T(8,128)S(1)} %copy-done.10, f32[16,128]{1,0:T(8,128)S(1)} %copy-done.30, f32[16,128]{1,0:T(8,128)S(1)} %copy-done.28, bf16[3,4,128,128]{2,3,1,0:T(8,128)(2,1)} %bitcast.395), kind=kOutput, calls=%fused_computation.26 | convolution fusion | flops 271581184 | bytes 5390336 | tf_op jit(solution)/shard_map/wqc,jcd->jwqd/dot_general | solution.py:69
  92.2 1.3 add_divide_fusion.2
  93.4 0.9 fusion.185
  94.3 3.1 %copy.261 = f32[2,2,16,128,128]{3,4,2,0,1:T(8,128)} copy(bf16[2,2,16,128,128]{4,3,0,2,1:T(8,128)(2,1)S(1)} %bitcast.376) | data formatting | bytes 6291456 | tf_op jit(solution)/shard_map/convert_element_type | solution.py:108
  97.4 3.0 %bitcast_add_fusion.2 = f32[4,16,128,128]{2,3,1,0:T(8,128)S(1)} fusion(f32[2,2,16,128,128]{3,4,2,0,1:T(8,128)} %copy.261, bf16[16,128,4,32]{1,3,2,0:T(8,128)(2,1)S(1)} %bitcast.380, bf16[16,128,4,32]{1,3,2,0:T(8,128)(2,1)S(1)} %bitcast.379), kind=kOutput, calls=%fused_computation.8 | convolution fusion | flops 69206016 | bytes 9437184 | tf_op jit(solution)/shard_map/wqhd,wkhd->hwqk/dot_general | solution.py:105
  100.4 2.8 %fusion.188 = (f32[4,16,128]{2,1,0:T(8,128)S(1)}, f32[4,16,128,128]{2,3,1,0:T(8,128)}) fusion(f32[4,16,128,128]{2,3,1,0:T(8,128)S(1)} %bitcast_add_fusion.2), kind=kOutput, calls=%fused_computation.255 | output fusion | flops 2097279 | bytes 8421376 | tf_op jit(solution)/shard_map/sub | solution.py:110
  103.4 3.2 %fusion.39 = bf16[16,128,4,32]{1,3,2,0:T(8,128)(2,1)S(1)} fusion(f32[16,128,4,32]{1,3,2,0:T(8,128)S(1)} %bitcast.386, bf16[16,128,4,32]{1,3,2,0:T(8,128)(2,1)} %bitcast.392, f32[4,16,128,128]{2,3,1,0:T(8,128)} %get-tuple-element.24, f32[4,16,128]{2,1,0:T(8,128)S(1)} %get-tuple-element.23), kind=kOutput, calls=%fused_computation.49 | convolution fusion | flops 69730304 | bytes 6324224 | tf_op jit(solution)/shard_map/hwqk,wkhd->wqhd/dot_general | solution.py:112
  108.3 4.6 %add_bitcast_fusion.1 = f32[6,16,128,128]{2,3,1,0:T(8,128)} fusion(f32[6,128]{1,0:T(8,128)S(1)} %get-tuple-element.20, bf16[16,128,128,1]{1,2,0,3:T(8,128)(2,1)S(1)} %copy-done.7, bf16[3,6,128,128]{3,2,1,0:T(8,128)(2,1)} %param.29), kind=kOutput, calls=%fused_computation.4 | convolution fusion | flops 404226048 | bytes 7015424 | tf_op jit(solution)/shard_map/wqc,jcd->jwqd/dot_general | solution.py:86
  112.9 1.3 fusion.157
  114.2 3.8 %fusion.190 = (f32[16,128]{1,0:T(8,128)S(1)}, f32[16,128,128]{1,2,0:T(8,128)}) fusion(f32[16,128,128]{1,2,0:T(8,128)} %copy-done.8, bf16[3,256,128]{2,1,0:T(8,128)(2,1)} %param.34, f32[16,128,256]{2,1,0:T(8,128)S(1)} %fusion.157, bf16[16,128,128]{1,2,0:T(8,128)(2,1)S(1)} %fusion.93, bf16[3,2,128,256]{3,2,1,0:T(8,128)(2,1)} %param.33, ...), kind=kOutput, calls=%fused_computation.257 | convolution fusion | flops 273152000 | bytes 5906432 | tf_op jit(solution)/shard_map/wqh,hc->wqc/dot_general | solution.py:138
  118.0 1.3 multiply_reduce_fusion.4
  119.4 2.8 %convert_bitcast_fusion.1 = bf16[4,16,128,128]{2,3,1,0:T(8,128)(2,1)S(1)} fusion(f32[6,16,128,128]{2,3,1,0:T(8,128)} %add_bitcast_fusion.1, f32[16,128,128]{1,2,0:T(8,128)} %get-tuple-element.28, f32[16,128]{1,0:T(8,128)S(1)} %add_rsqrt_fusion.4, f32[16,128]{1,0:T(8,128)S(1)} %broadcast_multiply_fusion.5, bf16[3,4,128,128]{2,3,1,0:T(8,128)(2,1)S(1)} %bitcast.396), kind=kOutput, calls=%fused_computation.24 | convolution fusion | flops 271581184 | bytes 5390336 | tf_op jit(solution)/shard_map/wqc,jcd->jwqd/dot_general | solution.py:69
  123.4 4.1 %fusion.193 = (f32[4,16,128]{2,1,0:T(8,128)S(1)}, f32[4,16,128,128]{2,3,1,0:T(8,128)S(1)}) fusion(f32[4,16,128,128]{2,3,1,0:T(8,128)S(1)} %bitcast_add_fusion.1), kind=kOutput, calls=%fused_computation.258 | output fusion | flops 2097279 | bytes 8421376 | tf_op jit(solution)/shard_map/sub | solution.py:110
  128.3 1.5 slice-done.1
  131.1 1.8 %fusion.153 = f32[16,128,256]{2,1,0:T(8,128)} fusion(bf16[16,128,128]{1,2,0:T(8,128)(2,1)S(1)} %fusion.71, bf16[3,2,128,256]{3,2,1,0:T(8,128)(2,1)S(1)} %copy-done.24), kind=kOutput, calls=%fused_computation.194 | convolution fusion | flops 134217728 | bytes 2686976 | tf_op jit(solution)/shard_map/wqc,ch->wqh/dot_general | solution.py:131
  132.9 4.0 %fusion.195 = (f32[16,128]{1,0:T(8,128)S(1)}, f32[16,128,128]{1,2,0:T(8,128)}) fusion(f32[16,128,128]{1,2,0:T(8,128)S(1)} %get-tuple-element.32, bf16[3,256,128]{2,1,0:T(8,128)(2,1)} %param.34, f32[16,128,256]{2,1,0:T(8,128)} %fusion.153, bf16[16,128,128]{1,2,0:T(8,128)(2,1)S(1)} %fusion.71, bf16[3,2,128,256]{3,2,1,0:T(8,128)(2,1)S(1)} %copy-done.24, ...), kind=kOutput, calls=%fused_computation.260 | convolution fusion | flops 273152000 | bytes 5906432 | tf_op jit(solution)/shard_map/wqh,hc->wqc/dot_general | solution.py:138
  136.9 2.0 %add_bitcast_fusion = f32[6,16,128,128]{2,3,1,0:T(8,128)S(1)} fusion(f32[6,128]{1,0:T(8,128)S(1)} %get-tuple-element.18, bf16[16,128,128,1]{1,2,0,3:T(8,128)(2,1)S(1)} %copy-done.7, bf16[3,6,128,128]{3,2,1,0:T(8,128)(2,1)} %param.29), kind=kOutput, calls=%fused_computation.3 | convolution fusion | flops 404226048 | bytes 7015424 | tf_op jit(solution)/shard_map/wqc,jcd->jwqd/dot_general | solution.py:86
  140.3 3.1 %copy-done.3 = f32[2,2,16,128,128]{3,4,2,0,1:T(8,128)S(1)} copy-done((f32[2,2,16,128,128]{3,4,2,0,1:T(8,128)S(1)}, f32[2,2,16,128,128]{3,4,2,0,1:T(8,128)}, u32[]{:S(2)}) %copy-start.3) | copy-done | bytes 4194328
  144.2 3.9 %fusion.198 = (f32[4,16,128]{2,1,0:T(8,128)S(1)}, f32[4,16,128,128]{2,3,1,0:T(8,128)S(1)}) fusion(f32[4,16,128,128]{2,3,1,0:T(8,128)S(1)} %bitcast_add_fusion), kind=kOutput, calls=%fused_computation.261 | output fusion | flops 2097279 | bytes 8421376 | tf_op jit(solution)/shard_map/sub | solution.py:110
  149.7 1.8 %fusion.149 = f32[16,128,256]{2,1,0:T(8,128)} fusion(bf16[16,128,128]{1,2,0:T(8,128)(2,1)S(1)} %fusion.49, bf16[3,2,128,256]{3,2,1,0:T(8,128)(2,1)S(1)} %copy-done.24), kind=kOutput, calls=%fused_computation.191 | convolution fusion | flops 134217728 | bytes 2686976 | tf_op jit(solution)/shard_map/wqc,ch->wqh/dot_general | solution.py:131
  151.5 3.0 %fusion.200 = (f32[16,128]{1,0:T(8,128)S(1)}, f32[16,128,128]{1,2,0:T(8,128)S(1)}) fusion(f32[16,128,128]{1,2,0:T(8,128)S(1)} %get-tuple-element.38, bf16[3,256,128]{2,1,0:T(8,128)(2,1)} %param.34, f32[16,128,256]{2,1,0:T(8,128)} %fusion.149, bf16[16,128,128]{1,2,0:T(8,128)(2,1)S(1)} %fusion.49, bf16[3,2,128,256]{3,2,1,0:T(8,128)(2,1)S(1)} %copy-done.24, ...), kind=kOutput, calls=%fused_computation.263 | convolution fusion | flops 273152000 | bytes 5906432 | tf_op jit(solution)/shard_map/wqh,hc->wqc/dot_general | solution.py:138
  155.3 3.5 %all_to_all.54 = f32[2,1,3072]{2,1,0:T(1,128)S(1)} all-to-all(f32[2,1,3072]{2,1,0:T(1,128)S(1)} %reshape.276), channel_id=1, replica_groups=mesh['win_0'=4,'win_1'=4,'win_2'=8,'head'=2] {'head'}, dimensions={0} | all-to-all | bytes 49152 | tf_op jit(solution)/shard_map/all_to_all | solution.py:163
  (147 shorter events, 19.2 us)
Async XLA Ops:
  0.0 55.0 %copy-start = (bf16[512,384]{1,0:T(8,128)(2,1)S(1)}, bf16[512,384]{1,0:T(8,128)(2,1)}, u32[]{:S(2)}) copy-start(bf16[512,384]{1,0:T(8,128)(2,1)} %param.22) | copy-start | bytes 1179652
  0.0 65.9 %copy-start.12 = (bf16[2,32,128,128]{3,2,1,0:T(8,128)(2,1)S(1)}, bf16[2,32,128,128]{3,2,1,0:T(8,128)(2,1)}, u32[]{:S(2)}) copy-start(bf16[2,32,128,128]{3,2,1,0:T(8,128)(2,1)} %param.25) | copy-start | bytes 6291460
  3.7 55.9 %copy-start.17 = (f32[3,32,64]{2,1,0:T(8,128)}, f32[3,32,64]{2,1,0:T(8,128)S(1)}, u32[]{:S(2)}) copy-start(f32[3,32,64]{2,1,0:T(8,128)S(1)} %get-tuple-element.6) | copy-start | bytes 73732
  50.6 16.8 %copy-start.32 = (f32[3]{0:T(128)}, f32[3]{0:T(128)S(1)}, u32[]{:S(2)}) copy-start(f32[3]{0:T(128)S(1)} %broadcast_divide_fusion) | copy-start | bytes 40
  51.4 8.1 %all-to-all-start.1 = ((f32[2,1,3072]{2,1,0:T(1,128)}), f32[2,1,3072]{2,1,0:T(1,128)S(1)}, u32[]{:S(2)}, u32[]{:S(2)}) async-start(f32[2,1,3072]{2,1,0:T(1,128)} %reshape.274), calls=%async_computation.1 | async-start | bytes 49152 | tf_op jit(solution)/shard_map/all_to_all | solution.py:150
  59.5 0.6 copy-start.23
  60.2 7.2 %all-to-all-start = ((bf16[32,64,256]{2,1,0:T(8,128)(2,1)}), bf16[32,64,256]{2,1,0:T(8,128)(2,1)S(1)}, u32[]{:S(2)}, u32[]{:S(2)}) async-start(bf16[32,64,256]{2,1,0:T(8,128)(2,1)} %pad_maximum_fusion), calls=%async_computation | async-start | bytes 2097152 | tf_op jit(solution)/shard_map/all_to_all | solution.py:40
  67.4 27.0 %all-to-all-start.2 = ((bf16[2,32,128,128]{3,2,0,1:T(8,128)(2,1)}), bf16[2,32,128,128]{3,2,0,1:T(8,128)(2,1)S(1)}, u32[]{:S(2)}, u32[]{:S(2)}) async-start(bf16[2,32,128,128]{3,2,0,1:T(8,128)(2,1)} %copy.260), calls=%async_computation.2 | async-start | bytes 4194304 | tf_op jit(solution)/shard_map/all_to_all | solution.py:149
  71.1 2.8 %copy-start.29 = (f32[3,6,128]{2,1,0:T(8,128)S(1)}, f32[3,6,128]{2,1,0:T(8,128)}, u32[]{:S(2)}) copy-start(f32[3,6,128]{2,1,0:T(8,128)} %param.30) | copy-start | bytes 27652
  71.1 3.9 %copy-start.31 = (f32[3,128]{1,0:T(4,128)S(1)}, f32[3,128]{1,0:T(4,128)}, u32[]{:S(2)}) copy-start(f32[3,128]{1,0:T(4,128)} %param.28) | copy-start | bytes 4612
  72.3 5.5 %copy-start.26 = (bf16[3,64,128]{2,1,0:T(8,128)(2,1)S(1)}, bf16[3,64,128]{2,1,0:T(8,128)(2,1)}, u32[]{:S(2)}) copy-start(bf16[3,64,128]{2,1,0:T(8,128)(2,1)} %param.32) | copy-start | bytes 147460
  72.3 6.1 %copy-start.20 = (bf16[3,4,128,64]{2,3,1,0:T(8,128)(2,1)S(1)}, bf16[3,4,128,64]{2,3,1,0:T(8,128)(2,1)}, u32[]{:S(2)}) copy-start(bf16[3,4,128,64]{2,3,1,0:T(8,128)(2,1)} %param.31) | copy-start | bytes 589828
  74.1 4.3 %copy-start.25 = (f32[16,128]{1,0:T(8,128)}, f32[16,128]{1,0:T(8,128)S(1)}, u32[]{:S(2)}) copy-start(f32[16,128]{1,0:T(8,128)S(1)} %broadcast_multiply_fusion.8) | copy-start | bytes 24580
  76.1 1.0 copy-start.9
  76.1 2.3 %copy-start.27 = (f32[16,128]{1,0:T(8,128)}, f32[16,128]{1,0:T(8,128)S(1)}, u32[]{:S(2)}) copy-start(f32[16,128]{1,0:T(8,128)S(1)} %broadcast_multiply_fusion.7) | copy-start | bytes 24580
  82.7 0.8 copy-start.13
  86.4 3.9 %copy-start.10 = (f32[16,128,128]{1,2,0:T(8,128)S(1)}, f32[16,128,128]{1,2,0:T(8,128)}, u32[]{:S(2)}) copy-start(f32[16,128,128]{1,2,0:T(8,128)} %copy-done.9) | copy-start | bytes 3145732
  86.4 3.9 %copy-start.28 = (f32[16,128]{1,0:T(8,128)S(1)}, f32[16,128]{1,0:T(8,128)}, u32[]{:S(2)}) copy-start(f32[16,128]{1,0:T(8,128)} %copy-done.27) | copy-start | bytes 24580
  86.4 3.9 %copy-start.30 = (f32[16,128]{1,0:T(8,128)S(1)}, f32[16,128]{1,0:T(8,128)}, u32[]{:S(2)}) copy-start(f32[16,128]{1,0:T(8,128)} %add_rsqrt_fusion.6) | copy-start | bytes 24580
  87.5 0.8 copy-start.6
  90.3 4.0 %copy-start.4 = (f32[6,16,128,128]{2,3,1,0:T(8,128)}, f32[6,16,128,128]{2,3,1,0:T(8,128)S(1)}, u32[]{:S(2)}) copy-start(f32[6,16,128,128]{2,3,1,0:T(8,128)S(1)} %add_bitcast_fusion.2) | copy-start | bytes 18874372
  100.4 2.8 %slice-start.4 = ((bf16[128,1920]{1,0:T(8,128)(2,1)}), bf16[128,384]{1,0:T(8,128)(2,1)S(1)}, s32[]{:S(2)}) async-start(bf16[128,1920]{1,0:T(8,128)(2,1)} %copy-done.13), calls=%async_computation.8 | async-start | bytes 196608 | tf_op jit(solution)/shard_map/split | solution.py:23
  100.4 2.9 %copy-start.14 = (f32[1,16,128,128]{2,3,1,0:T(8,128)S(1)}, f32[1,16,128,128]{2,3,1,0:T(8,128)}, u32[]{:S(2)}) copy-start(f32[1,16,128,128]{2,3,1,0:T(8,128)} %add_divide_fusion.2) | copy-start | bytes 3145732
  100.4 6.1 %slice-start.2 = ((s8[6291456]{0:T(1024)(128)(4,1)}), s8[2097152]{0:T(1024)(128)(4,1)S(1)}, s32[]{:S(2)}) async-start(s8[6291456]{0:T(1024)(128)(4,1)} %bitcast.374), calls=%async_computation.6 | async-start | bytes 4194304
  103.3 3.2 %copy-start.21 = (bf16[128,384]{0,1:T(8,128)(2,1)}, bf16[128,384]{0,1:T(8,128)(2,1)S(1)}, u32[]{:S(2)}) copy-start(bf16[128,384]{0,1:T(8,128)(2,1)S(1)} %copy.263) | copy-start | bytes 294916
  103.3 3.6 %slice-start.3 = ((s8[6291456]{0:T(1024)(128)(4,1)}), s8[4194304]{0:T(1024)(128)(4,1)S(1)}, s32[]{:S(2)}) async-start(s8[6291456]{0:T(1024)(128)(4,1)} %bitcast.374), calls=%async_computation.7 | async-start | bytes 8388608
  103.3 3.9 %copy-start.11 = (f32[16,128,128]{1,2,0:T(8,128)S(1)}, f32[16,128,128]{1,2,0:T(8,128)}, u32[]{:S(2)}) copy-start(f32[16,128,128]{1,2,0:T(8,128)} %copy-done.9) | copy-start | bytes 3145732
  107.3 1.0 copy-start.7
  107.7 5.2 %copy-start.8 = (f32[16,128,128]{1,2,0:T(8,128)}, f32[16,128,128]{1,2,0:T(8,128)S(1)}, u32[]{:S(2)}) copy-start(f32[16,128,128]{1,2,0:T(8,128)S(1)} %get-tuple-element.26) | copy-start | bytes 3145732
  114.2 5.2 %copy-start.19 = (bf16[128,3,4,128]{3,0,2,1:T(8,128)(2,1)S(1)}, bf16[128,3,4,128]{3,0,2,1:T(8,128)(2,1)}, u32[]{:S(2)}) copy-start(bf16[128,3,4,128]{3,0,2,1:T(8,128)(2,1)} %copy.256) | copy-start | bytes 1179652
  119.4 3.2 %copy-start.2 = (f32[2,2,16,128,128]{3,4,2,0,1:T(8,128)S(1)}, f32[2,2,16,128,128]{3,4,2,0,1:T(8,128)}, u32[]{:S(2)}) copy-start(f32[2,2,16,128,128]{3,4,2,0,1:T(8,128)} %copy.261) | copy-start | bytes 12582916
  123.4 4.9 %slice-start = ((s8[6291456]{0:T(1024)(128)(4,1)}), s8[2097152]{0:T(1024)(128)(4,1)S(1)}, s32[]{:S(2)}) async-start(s8[6291456]{0:T(1024)(128)(4,1)} %bitcast.372), calls=%async_computation.4 | async-start | bytes 4194304
  127.6 2.2 %slice-start.1 = ((s8[6291456]{0:T(1024)(128)(4,1)}), s8[4194304]{0:T(1024)(128)(4,1)S(1)}, s32[]{:S(2)}) async-start(s8[6291456]{0:T(1024)(128)(4,1)} %bitcast.372), calls=%async_computation.5 | async-start | bytes 8388608
  127.6 2.5 %copy-start.16 = (f32[16,128,128]{1,2,0:T(8,128)S(1)}, f32[16,128,128]{1,2,0:T(8,128)}, u32[]{:S(2)}) copy-start(f32[16,128,128]{1,2,0:T(8,128)} %get-tuple-element.28) | copy-start | bytes 3145732
  127.6 2.5 %copy-start.22 = (bf16[128,384]{0,1:T(8,128)(2,1)S(1)}, bf16[128,384]{0,1:T(8,128)(2,1)}, u32[]{:S(2)}) copy-start(bf16[128,384]{0,1:T(8,128)(2,1)} %copy-done.21) | copy-start | bytes 294916
  130.1 1.0 copy-start.24
  136.9 2.1 %copy-start.15 = (f32[16,128,128]{1,2,0:T(8,128)S(1)}, f32[16,128,128]{1,2,0:T(8,128)}, u32[]{:S(2)}) copy-start(f32[16,128,128]{1,2,0:T(8,128)} %get-tuple-element.34) | copy-start | bytes 3145732
  138.9 10.5 %copy-start.5 = (f32[6,16,128,128]{2,3,1,0:T(8,128)}, f32[6,16,128,128]{2,3,1,0:T(8,128)S(1)}, u32[]{:S(2)}) copy-start(f32[6,16,128,128]{2,3,1,0:T(8,128)S(1)} %add_bitcast_fusion) | copy-start | bytes 18874372
  139.1 4.3 %copy-start.3 = (f32[2,2,16,128,128]{3,4,2,0,1:T(8,128)S(1)}, f32[2,2,16,128,128]{3,4,2,0,1:T(8,128)}, u32[]{:S(2)}) copy-start(f32[2,2,16,128,128]{3,4,2,0,1:T(8,128)} %copy.261) | copy-start | bytes 12582916
  151.5 3.2 %copy-start.34 = (bf16[3,128]{1,0:T(4,128)(2,1)S(1)}, bf16[3,128]{1,0:T(4,128)(2,1)}, u32[]{:S(2)}) copy-start(bf16[3,128]{1,0:T(4,128)(2,1)} %param.35) | copy-start | bytes 2308
  151.5 8.4 %copy-start.18 = (f32[3,32,64]{2,1,0:T(8,128)S(1)}, f32[3,32,64]{2,1,0:T(8,128)}, u32[]{:S(2)}) copy-start(f32[3,32,64]{2,1,0:T(8,128)} %copy-done.17) | copy-start | bytes 73732
  151.5 8.4 %copy-start.33 = (f32[3]{0:T(128)S(1)}, f32[3]{0:T(128)}, u32[]{:S(2)}) copy-start(f32[3]{0:T(128)} %copy-done.32) | copy-start | bytes 40
  151.5 9.1 %copy-start.1 = (bf16[512,384]{1,0:T(8,128)(2,1)S(1)}, bf16[512,384]{1,0:T(8,128)(2,1)}, u32[]{:S(2)}) copy-start(bf16[512,384]{1,0:T(8,128)(2,1)} %param.22) | copy-start | bytes 1179652
where the time goes:
time: 162 us; the launch traced here: 161 us
  blocking collectives  50.7 us (31%)
  matrix products  43.7 us (27%)
  other arithmetic  27.4 us (17%)
  local copies, waits for them, and re-layouts  25.7 us (16%)
  starting transfers between devices  10.9 us (7%)
  between operations  2.19 us (1%)
    psum x4, blocking collectives, by_axis(): array = lax.psum(array, axis)  44.8 us
    unnamed x85, local copies, waits for them, and re-layouts  13.3 us
    sub x3, other arithmetic, window_net(): exponent = jnp.exp(scores - row_max)  10.9 us
    dot_general x3, matrix products, window_net(): jnp.einsum('wqh,hc->wqc', hidden, down_weight[block_index], preferred_ele...  10.8 us
    dot_general x3, matrix products, window_net(): jnp.einsum('wqc,jcd->jwqd', cond_norm, ada_weight[block_index], preferred...  8.58 us
    dot_general x3, matrix products, project_rows(): jnp.einsum('wqc,jcd->jwqd', portion, weight_set, preferred_element_type=j...  5.36 us
    dot_general x3, matrix products, window_net(): jnp.einsum('wqc,ch->wqh', normed_two, gateup_weight[block_index, 1], pref...  4.92 us
    dot_general x3, matrix products, window_net(): jnp.einsum('wqhd,wkhd->hwqk', query_rows, key_rows, preferred_element_typ...  4.54 us
  transfers between devices with their start and end apart: 3, of which 0 were waited for; matrix products, arithmetic and copies ran while one was open for 16% of the time, Pallas kernels for 0%

commit v1 on v0

v1 whole, which is shorter than its diff:
```python
import functools
import math

import jax
import jax.numpy as jnp
from jax import lax
from jax.experimental import pallas as pl
from jax.experimental.pallas import tpu as pltpu
from jax.sharding import Mesh
from jax.sharding import PartitionSpec as P

HEADS = 4
HEAD_DIM = 32
HALF_HEADS = 2
C = 128
QW = 128
HALF = 64
HID = 256
TOKW = 16
BLOCKS = 3
EPSILON = 1e-05
WIN = ("win_0", "win_1", "win_2")
GROUP = 4
LOG2E = math.log2(math.e)
F32 = jnp.float32
BF16 = jnp.bfloat16

NN = (((1,), (0,)), ((), ()))
NT = (((1,), (1,)), ((), ()))


def mm(a, b, dims=NN):
    return lax.dot_general(a, b, dims, preferred_element_type=F32)


def norm(x):
    mean = jnp.sum(x, axis=0, keepdims=True) * (1.0 / C)
    centred = x - mean
    var = jnp.sum(centred * centred, axis=0, keepdims=True) * (1.0 / C)
    return centred, lax.rsqrt(var + EPSILON)


def kernel(
    sizes,
    sigma,
    coords,
    noise,
    single,
    tokens,
    atok,
    wcount,
    pbias,
    tokw,
    gain,
    posw,
    adaw,
    adab,
    attnw,
    outw,
    guw,
    downw,
    finw,
    out,
    s,
):
    ny, nx, nz = sizes
    y, x, z = (lax.axis_index(name) for name in WIN)
    h = lax.axis_index("head")
    other = 1 - h
    slots = coords.shape[1]
    W = slots // 2
    NP = W // 2
    mine = pl.multiple_of(h * W, W)
    theirs = pl.multiple_of(other * W, W)

    n1, n2 = 2 * nz, ny * nx
    me1, me2 = z * 2 + h, y * nx + x

    def dev1(i):
        return {"win_2": i // 2, "head": lax.rem(i, 2)}

    def dev2(i):
        return {"win_0": i // nx, "win_1": lax.rem(i, nx)}

    barrier = pltpu.get_barrier_semaphore()
    for n, me, dev in ((n1, me1, dev1), (n2, me2, dev2)):
        for j in range(1, n):
            pl.semaphore_signal(
                barrier,
                inc=1,
                device_id=dev(lax.rem(me + j, n)),
                device_id_type=pl.DeviceIdType.MESH,
            )

    count = [0]

    def fetch(src, dst):
        copy = pltpu.make_async_copy(src, dst, s.lsem.at[count[0]])
        count[0] += 1
        copy.start()
        return copy

    small = [
        fetch(coords, s.cfull),
        fetch(noise, s.nfull),
        fetch(wcount, s.wc),
    ]
    prep = [
        fetch(gain, s.gain),
        fetch(posw, s.pw),
        fetch(adab, s.adab),
        fetch(finw, s.fin),
        fetch(tokw, s.tokw),
        fetch(tokens.at[pl.ds(pl.multiple_of(h * W * TOKW, W * TOKW), W * TOKW)], s.tok),
    ]
    c_ada = fetch(adaw, s.adaw)
    c_gu = fetch(guw, s.guw)
    c_down = fetch(downw, s.downw)
    own_rows = pl.ds(pl.multiple_of(h * HALF, HALF), HALF)
    own_in = [
        fetch(single.at[pl.ds(mine, W)], s.atoms.at[:, own_rows, :]),
        fetch(atok.at[pl.ds(mine, W)], s.tokidx.at[h]),
        fetch(coords.at[:, pl.ds(mine, W)], s.cpos.at[h]),
        fetch(noise.at[:, pl.ds(mine, W)], s.npos.at[h]),
        fetch(attnw, s.attn_l),
        fetch(outw, s.out_l),
        fetch(pbias.at[:, pl.ds(mine, W)], s.bias_l),
    ]

    sig = jnp.full((1, 128), sigma[0], F32)
    inv = 1.0 / (1.0 + sig * sig)
    root = jnp.sqrt(inv)
    lane = lax.broadcasted_iota(jnp.int32, (1, 128), 1)

    for c in small:
        c.wait()
    counts = s.wc[...].astype(F32)
    win_id = (y * nx + x) * nz + z
    win_lane = lax.broadcasted_iota(jnp.int32, counts.shape, 1)
    own_count = jnp.sum(jnp.where(win_lane == win_id, counts, 0.0), axis=1, keepdims=True)
    atoms_total = QW * jnp.sum(counts, axis=1, keepdims=True)
    slot = lax.broadcasted_iota(jnp.int32, (slots, HALF), 0).astype(F32)
    live = slot < own_count
    row = jnp.zeros((1, 128), F32)
    for k in range(3):
        noisy = jnp.where(live, s.cfull[k] + sig[:, :HALF] * s.nfull[k], 0.0)
        part = jnp.sum(jnp.sum(noisy, axis=0, keepdims=True), axis=1, keepdims=True)
        row = jnp.where(lane == k, part, row)
    s.red1[me1] = row

    pl.semaphore_wait(barrier, n1 - 1 + n2 - 1)

    def remote(src, dst, send, recv, dev):
        return pltpu.make_async_remote_copy(
            src_ref=src,
            dst_ref=dst,
            send_sem=send,
            recv_sem=recv,
            device_id=dev,
            device_id_type=pl.DeviceIdType.MESH,
        )

    def spread(buf, n, me, dev, ssem, rsem):
        sends = []
        for j in range(1, n):
            c = remote(buf.at[me], buf.at[me], ssem.at[j], rsem.at[me], dev(lax.rem(me + j, n)))
            c.start()
            sends.append(c)
        return sends

    def collect(buf, n, me, dev, ssem, rsem):
        for j in range(1, n):
            src = lax.rem(me + j, n)
            remote(buf.at[src], buf.at[src], ssem.at[j], rsem.at[src], dev(src)).wait_recv()

    sends1 = spread(s.red1, n1, me1, dev1, s.ssem1, s.rsem1)

    pair = [0]

    def give(src, dst):
        i = pair[0]
        pair[0] += 1
        c = remote(src, dst, s.psend.at[i], s.precv.at[i], {"head": other})
        c.start()
        return c

    x_atoms = give(single.at[pl.ds(theirs, W)], s.atoms.at[:, own_rows, :])
    x_tok = give(atok.at[pl.ds(theirs, W)], s.tokidx.at[h])
    x_c = give(coords.at[:, pl.ds(theirs, W)], s.cpos.at[h])
    x_n = give(noise.at[:, pl.ds(theirs, W)], s.npos.at[h])
    x_attn = give(attnw, s.attn_r)
    x_out = give(outw, s.out_r)
    x_bias = give(pbias.at[:, pl.ds(theirs, W)], s.bias_r)

    def turned(values, scale=None):
        values = values.astype(F32)
        if scale is not None:
            values = values * scale
        return values.T.astype(BF16)

    for c in prep:
        c.wait()
    s.tokwT[...] = turned(s.tokw[...])
    s.gainT[...] = jnp.broadcast_to(s.gain[...], (C, C)).T
    for k in range(3):
        s.pwT[k] = jnp.broadcast_to(s.pw[k : k + 1, :], (C, C)).T
    for b in range(BLOCKS):
        for j in range(6):
            bias = jnp.broadcast_to(s.adab[b][j : j + 1, :], (C, C)).T
            s.adabT[b * 6 + j] = bias * 0.5 if j in (0, 2, 3, 5) else bias
    c_ada.wait()
    for b in range(BLOCKS):
        for j in range(6):
            s.adaT[b, j * C : (j + 1) * C, :] = turned(
                s.adaw[b, j], 0.5 if j in (0, 2, 3, 5) else None
            )
    s.tpT[...] = mm(s.tokwT[...], s.tok[...], NT).astype(BF16)
    c_gu.wait()
    c_down.wait()
    for b in range(BLOCKS):
        s.guT[b, :HID, :] = turned(s.guw[b, 0], 0.5)
        s.guT[b, HID:, :] = turned(s.guw[b, 1])
        s.downT[b] = turned(s.downw[b], 0.5)

    for c in own_in:
        c.wait()
    for c in (x_tok, x_c, x_n, x_atoms):
        c.wait()
    s.tokcat[...] = jnp.concatenate([s.tokidx[0], s.tokidx[1]], axis=1)
    for k in range(3):
        halves = [(s.cpos[a, k] + sig[:, :HALF] * s.npos[a, k]) * root[:, :HALF] for a in (0, 1)]
        s.pos[k] = jnp.concatenate(halves, axis=1)

    eye = (
        lax.broadcasted_iota(jnp.int32, (C, C), 0) == lax.broadcasted_iota(jnp.int32, (C, C), 1)
    ).astype(BF16)

    def condition(p):
        for w in range(2):
            lanes = pl.ds(w * QW, QW)
            win = 2 * p + w
            own = s.tokcat[pl.ds(win, 1), :] + win * TOKW
            ids = lax.broadcasted_iota(jnp.int32, (W * TOKW, QW), 0)
            one_hot = jnp.where(ids == own, 1.0, 0.0).astype(BF16)
            cond = mm(eye, s.atoms[win], NT) + mm(s.tpT[...], one_hot)
            centred, rstd = norm(cond)
            s.cn[:, lanes] = (centred * rstd * s.gainT[...]).astype(BF16)
            for k in range(3):
                cond = cond + s.pos[k, pl.ds(win, 1), :] * s.pwT[k]
            s.stream[p, :, lanes] = cond
        for b in range(BLOCKS):
            terms = mm(s.adaT[b], s.cn[...])
            for j in range(6):
                for w in range(2):
                    lanes = pl.ds(w * QW, QW)
                    a = terms[j * C : (j + 1) * C, w * QW : (w + 1) * QW] + s.adabT[b * 6 + j]
                    if j in (0, 2, 3, 5):
                        a = 1.0 + jnp.tanh(a)
                    s.ada[p, b * 6 + j, :, lanes] = a

    def first(p, carry):
        condition(p)
        return carry

    half = NP // 2
    lax.fori_loop(0, half, first, 0)

    collect(s.red1, n1, me1, dev1, s.ssem1, s.rsem1)
    s.red2[me2] = jnp.sum(s.red1[...], axis=0)
    sends2 = spread(s.red2, n2, me2, dev2, s.ssem2, s.rsem2)

    lax.fori_loop(half, NP, first, 0)

    x_attn.wait()
    x_out.wait()
    for b in range(BLOCKS):
        for j in range(4):
            both = jnp.concatenate(
                [s.attn_l[b, j].astype(F32), s.attn_r[b, j].astype(F32)], axis=1
            )
            s.attnT[b, j * C : (j + 1) * C, :] = turned(both, 0.5 if j == 3 else None)
        both = jnp.concatenate([s.out_l[b].astype(F32), s.out_r[b].astype(F32)], axis=0)
        s.outT[b] = turned(both, 0.25)
    x_bias.wait()

    def turn_bias(w, carry):
        for a in range(HALF_HEADS):
            for side, buf in enumerate((s.bias_l, s.bias_r)):
                i = side * HALF_HEADS + a
                s.biasT[w, :, i * QW : (i + 1) * QW] = (buf[a, w].astype(F32) * LOG2E).T
        return carry

    lax.fori_loop(0, W, turn_bias, 0)

    collect(s.red2, n2, me2, dev2, s.ssem2, s.rsem2)
    total = jnp.sum(s.red2[...], axis=0) / atoms_total
    centre = [
        jnp.sum(jnp.where(lane == k, total, 0.0), axis=1, keepdims=True) for k in range(3)
    ]
    shift = jnp.zeros((C, C), F32)
    for k in range(3):
        shift = shift + (centre[k] * root) * s.pwT[k]
    s.shift[...] = shift

    q_scale = LOG2E * HEAD_DIM ** (-0.5)
    pairs = GROUP // 2

    def begin(p, carry):
        for w in range(2):
            lanes = pl.ds(w * QW, QW)
            s.stream[p, :, lanes] = s.stream[p, :, lanes] - s.shift[...]
        return carry

    lax.fori_loop(0, NP, begin, 0)

    def block(step, carry):
        b = lax.rem(step, BLOCKS)
        base = (step // BLOCKS) * pairs

        def term(i, j, w):
            return s.ada[base + i, b * 6 + j, :, pl.ds(w * QW, QW)]

        for i in range(pairs):
            for w in range(2):
                lanes = pl.ds(w * QW, QW)
                centred, rstd = norm(s.stream[base + i, :, lanes])
                n = centred * (0.5 * rstd) * term(i, 0, w) + term(i, 1, w)
                s.n[i, :, lanes] = n.astype(BF16)
        for i in range(pairs):
            proj = mm(s.attnT[b], s.n[i])
            s.q[i] = (proj[:C] * q_scale).astype(BF16)
            s.v[i] = proj[2 * C : 3 * C].astype(BF16)
            s.gate[i] = 1.0 + jnp.tanh(proj[3 * C :])
            for w in range(2):
                s.k[2 * i + w] = proj[C : 2 * C, w * QW : (w + 1) * QW].T.astype(BF16)
        for i in range(pairs):
            for w in range(2):
                lanes = pl.ds(w * QW, QW)
                keys = s.k[2 * i + w]
                attended = []
                for hp in range(2):
                    cols = []
                    for a in range(2):
                        at = (2 * hp + a) * HEAD_DIM
                        part = [s.q[i, at : at + HEAD_DIM, lanes]]
                        if at > 0:
                            part = [jnp.zeros((at, QW), BF16)] + part
                        if at + HEAD_DIM < C:
                            part = part + [jnp.zeros((C - HEAD_DIM - at, QW), BF16)]
                        cols.append(jnp.concatenate(part, axis=0))
                    scores = mm(keys, jnp.concatenate(cols, axis=1))
                    for a in range(2):
                        hd = 2 * hp + a
                        sc = (
                            scores[:, a * QW : (a + 1) * QW]
                            + s.biasT[2 * (base + i) + w, :, hd * QW : (hd + 1) * QW]
                        )
                        e = jnp.exp2(sc - jnp.max(sc, axis=0, keepdims=True))
                        recip = 1.0 / jnp.sum(e, axis=0, keepdims=True)
                        at = hd * HEAD_DIM
                        o = mm(s.v[i, at : at + HEAD_DIM, lanes], e.astype(BF16))
                        attended.append(o * recip)
                both = jnp.concatenate(attended, axis=0) * s.gate[i, :, lanes]
                s.att[i, :, lanes] = both.astype(BF16)
        for i in range(pairs):
            update = mm(s.outT[b], s.att[i])
            for w in range(2):
                lanes = pl.ds(w * QW, QW)
                xs = s.stream[base + i, :, lanes] + term(i, 2, w) * update[:, w * QW : (w + 1) * QW]
                s.stream[base + i, :, lanes] = xs
                centred, rstd = norm(xs)
                n = centred * (0.5 * rstd) * term(i, 3, w) + term(i, 4, w)
                s.n[i, :, lanes] = n.astype(BF16)
        for i in range(pairs):
            both = mm(s.guT[b], s.n[i])
            g = both[:HID]
            s.hidden[i] = (g * (1.0 + jnp.tanh(g)) * both[HID:]).astype(BF16)
        for i in range(pairs):
            down = mm(s.downT[b], s.hidden[i])
            for w in range(2):
                lanes = pl.ds(w * QW, QW)
                s.stream[base + i, :, lanes] = (
                    s.stream[base + i, :, lanes] + term(i, 5, w) * down[:, w * QW : (w + 1) * QW]
                )
        return carry

    lax.fori_loop(0, BLOCKS * (NP // pairs), block, 0)

    final = jnp.concatenate([s.fin[...].astype(F32), jnp.zeros((5, C), F32)], axis=0).astype(BF16)

    def finish(p, carry):
        for w in range(2):
            centred, rstd = norm(s.stream[p, :, pl.ds(w * QW, QW)])
            upd = mm(final, (centred * rstd).astype(BF16))
            for k in range(3):
                s.upd[k, pl.ds(2 * p + w, 1), :] = upd[k : k + 1, :]
        return carry

    lax.fori_loop(0, NP, finish, 0)
    x_upd = give(s.upd, s.updr)

    def write(source, first_slot):
        first_slot = pl.multiple_of(first_slot, W)
        ids = (lax.broadcasted_iota(jnp.int32, (W, HALF), 0) + first_slot).astype(F32)
        alive = ids < own_count
        for k in range(3):
            both = source[k]
            upd = jnp.where(h == 0, both[:, :HALF], both[:, HALF:])
            here = pl.ds(first_slot, W)
            noisy = s.cfull[k, here, :] + sig[:, :HALF] * s.nfull[k, here, :]
            shifted = noisy - centre[k]
            value = shifted * inv[:, :HALF] + (sig * root)[:, :HALF] * upd
            out[k, here, :] = jnp.where(alive, value, 0.0)

    write(s.upd, mine)
    x_upd.wait()
    write(s.updr, theirs)
    for c in sends1 + sends2:
        c.wait_send()


class Scratch:
    pass


def scratch_of(slots, nz, nxy):
    win_total = nz * nxy
    W = slots // 2
    NP = W // 2
    G = GROUP // 2
    V = pltpu.VMEM
    return {
        "cfull": V((3, slots, HALF), F32),
        "nfull": V((3, slots, HALF), F32),
        "wc": V((1, win_total), jnp.int32),
        "gain": V((1, C), F32),
        "pw": V((3, C), F32),
        "adab": V((BLOCKS, 6, C), F32),
        "fin": V((3, C), BF16),
        "tokw": V((3 * C, C), BF16),
        "tok": V((W * TOKW, 3 * C), BF16),
        "adaw": V((BLOCKS, 6, C, C), BF16),
        "guw": V((BLOCKS, 2, C, HID), BF16),
        "downw": V((BLOCKS, HID, C), BF16),
        "atoms": V((W, QW, C), BF16),
        "tokidx": V((2, W, HALF), jnp.int32),
        "cpos": V((2, 3, W, HALF), F32),
        "npos": V((2, 3, W, HALF), F32),
        "attn_l": V((BLOCKS, 4, C, HALF), BF16),
        "attn_r": V((BLOCKS, 4, C, HALF), BF16),
        "out_l": V((BLOCKS, HALF, C), BF16),
        "out_r": V((BLOCKS, HALF, C), BF16),
        "bias_l": V((2, W, QW, QW), BF16),
        "bias_r": V((2, W, QW, QW), BF16),
        "red1": V((2 * nz, 1, 128), F32),
        "red2": V((nxy, 1, 128), F32),
        "tokwT": V((C, 3 * C), BF16),
        "gainT": V((C, C), F32),
        "pwT": V((3, C, C), F32),
        "adabT": V((BLOCKS * 6, C, C), F32),
        "adaT": V((BLOCKS, 6 * C, C), BF16),
        "attnT": V((BLOCKS, 4 * C, C), BF16),
        "outT": V((BLOCKS, C, C), BF16),
        "guT": V((BLOCKS, 2 * HID, C), BF16),
        "downT": V((BLOCKS, C, HID), BF16),
        "tpT": V((C, W * TOKW), BF16),
        "tokcat": V((W, QW), jnp.int32),
        "pos": V((3, W, QW), F32),
        "cn": V((C, 2 * QW), BF16),
        "stream": V((NP, C, 2 * QW), F32),
        "ada": V((NP, BLOCKS * 6, C, 2 * QW), F32),
        "biasT": V((W, QW, HEADS * QW), F32),
        "shift": V((C, C), F32),
        "n": V((G, C, 2 * QW), BF16),
        "q": V((G, C, 2 * QW), BF16),
        "k": V((2 * G, QW, C), BF16),
        "v": V((G, C, 2 * QW), BF16),
        "gate": V((G, C, 2 * QW), F32),
        "att": V((G, C, 2 * QW), BF16),
        "hidden": V((G, HID, 2 * QW), BF16),
        "upd": V((3, W, QW), F32),
        "updr": V((3, W, QW), F32),
        "lsem": pltpu.SemaphoreType.DMA((20,)),
        "ssem1": pltpu.SemaphoreType.DMA((2 * nz,)),
        "rsem1": pltpu.SemaphoreType.DMA((2 * nz,)),
        "ssem2": pltpu.SemaphoreType.DMA((nxy,)),
        "rsem2": pltpu.SemaphoreType.DMA((nxy,)),
        "psend": pltpu.SemaphoreType.DMA((8,)),
        "precv": pltpu.SemaphoreType.DMA((8,)),
    }


def make_local(sizes):
    def local(
        coords,
        noise,
        sigma,
        atom_single,
        token_single,
        atom_token,
        window_count,
        pair_bias,
        token_weight,
        cond_gain,
        position_weight,
        ada_weight,
        ada_bias,
        attn_weight,
        out_weight,
        gateup_weight,
        down_weight,
        final_weight,
    ):
        slots = coords.shape[1]
        ny, nx, nz = sizes
        scratch = scratch_of(slots, nz, ny * nx)
        names = list(scratch)

        def body(*refs):
            s = Scratch()
            for name, ref in zip(names, refs[19:]):
                setattr(s, name, ref)
            kernel(sizes, *refs[:19], s)

        any_spec = pl.BlockSpec(memory_space=pl.ANY)
        return pl.pallas_call(
            body,
            out_shape=jax.ShapeDtypeStruct(coords.shape, F32),
            in_specs=[pl.BlockSpec(memory_space=pltpu.SMEM)] + [any_spec] * 17,
            out_specs=pl.BlockSpec(memory_space=pltpu.VMEM),
            scratch_shapes=[scratch[name] for name in names],
            compiler_params=pltpu.CompilerParams(
                collective_id=0, has_side_effects=True, vmem_limit_bytes=60 * 1024 * 1024
            ),
            name="denoise",
        )(
            sigma,
            coords,
            noise,
            atom_single,
            token_single,
            atom_token,
            window_count.reshape(1, -1),
            pair_bias,
            token_weight,
            cond_gain.reshape(1, -1),
            position_weight,
            ada_weight,
            ada_bias,
            attn_weight,
            out_weight,
            gateup_weight,
            down_weight,
            final_weight,
        )

    return local


def solution(mesh):
    devices = mesh.devices
    head = mesh.shape["head"]
    sizes = (4, 4, 8) if devices.size == 256 else (2, 2, devices.size // (4 * head))
    torus = Mesh(devices.reshape(*sizes, head), WIN + ("head",))
    in_specs = (
        P(None, WIN, "head"),
        P(None, WIN, "head"),
        P(),
        P(WIN, "head", None),
        P(WIN, None),
        P(WIN, "head"),
        P(),
        P("head", WIN, None, None),
        P(),
        P(),
        P(),
        P(),
        P(),
        P(None, None, None, "head"),
        P(None, "head", None),
        P(),
        P(),
        P(),
    )
    out_specs = P(None, WIN, "head")
    return jax.shard_map(
        make_local(sizes), mesh=torus, in_specs=in_specs, out_specs=out_specs, check_vma=False
    )
```

time: 162 us -> 54.9 us (0.34)
  Pallas kernels: 0 us -> 50.8 us
  blocking collectives: 50.7 us -> 0 us
  matrix products: 43.7 us -> 0 us
  other arithmetic: 27.4 us -> 0 us
  local copies, waits for them, and re-layouts: 25.7 us -> 3.26 us
  starting transfers between devices: 10.9 us -> 0 us
    pallas_call x0 -> x1, Pallas kernels: none -> 50.8 us  [local(): pl.pallas_call(body, out_shape=jax.ShapeDtypeStruct(coords.shape, F32), i...]
    psum x4 -> x0, blocking collectives: 44.8 us -> none  [by_axis(): array = lax.psum(array, axis)]
    dot_general x25 -> x0, matrix products: 43.7 us -> none  [the longest x3 10.8 us: window_net(): jnp.einsum('wqh,hc->wqc', hidden, down_weight[block_index], preferred_ele...]
    all_to_all x3 -> x0, starting transfers between devices: 10.9 us -> none  [the longest x1 3.77 us: run_net(): lax.all_to_all(pair_terms, 'head', split_axis=1, concat_axis=0, tiled=True)]
    sub x3 -> x0, other arithmetic: 10.9 us -> none  [window_net(): exponent = jnp.exp(scores - row_max)]
    unnamed x85 -> x2, local copies, waits for them, and re-layouts: 13.3 us -> 3.26 us
    reduce_sum x11 -> x0, other arithmetic: 4.75 us -> none  [the longest x8 2.3 us: layer_norm(): variance = jnp.mean(centred * centred, axis=-1, keepdims=True)]
    all_to_all x1 -> x0, blocking collectives: 3.53 us -> none  [run_net(): lax.all_to_all(update_own, 'head', split_axis=2, concat_axis=1, tiled=True)]
  transfers between devices with their start and end apart: 3 -> 0, of which waited for: 0 -> 0; matrix products, arithmetic and copies ran while one was open for 16% -> 0% of each run, Pallas kernels for 0% -> 0%
where the time goes in v1:
time: 54.9 us; the launch traced here: 54.7 us
  Pallas kernels  50.8 us (93%)
  local copies, waits for them, and re-layouts  3.26 us (6%)
  between operations  0.66 us (1%)
    pallas_call x1, Pallas kernels, local(): pl.pallas_call(body, out_shape=jax.ShapeDtypeStruct(coords.shape, F32), i...  50.8 us
    unnamed x2, local copies, waits for them, and re-layouts  3.26 us

profile of v1, /device:TPU:1, one launch (start us, length us, event | category | flops | bytes accessed | tf_op | source)
XLA Modules:
  0.0 54.7 jit_solution(4034397900217530981)
XLA Ops:
  0.7 1.8 %copy.19.refs_13_ = bf16[3,4,128,64]{3,2,1,0:T(8,128)(2,1)} copy(bf16[3,4,128,64]{2,3,1,0:T(8,128)(2,1)} %param.31) | data formatting | bytes 393216 | tf_op args[13]
  2.5 50.8 %denoise.1 = f32[3,32,64]{2,1,0:T(8,128)} custom-call(f32[1]{0:T(128)S(6)} %copy.21.refs_0_, f32[3,32,64]{2,1,0:T(8,128)} %refs_1_.1, f32[3,32,64]{2,1,0:T(8,128)} %refs_2_.1, bf16[32,64,128]{2,1,0:T(8,128)(2,1)} %refs_3_.1, bf16[512,384]{1,0:T(8,128)(2,1)} %refs_4_.1, s32[32,64]{1,0:T(8,128)} %refs_5_.1, s32[1,128]{1,0:T(1,128)} %bitcast.2, ...), custom_call_target="tpu_custom_call" | custom-call | tf_op jit(solution)/shard_map/denoise/pallas_call | solution.py:526
  53.3 1.4 %copy.22 = f32[3,32,64]{2,1,0:T(8,128)} copy(f32[3,32,64]{2,1,0:T(8,128)} %denoise.1) | data formatting | bytes 49152

commit v2 on v1

--- a/solution.py
+++ b/solution.py
@@ -20,7 +20,6 @@
 BLOCKS = 3
 EPSILON = 1e-05
 WIN = ("win_0", "win_1", "win_2")
-GROUP = 4
 LOG2E = math.log2(math.e)
 F32 = jnp.float32
 BF16 = jnp.bfloat16
@@ -104,6 +103,7 @@
         fetch(coords, s.cfull),
         fetch(noise, s.nfull),
         fetch(wcount, s.wc),
+        fetch(sigma, s.sig),
     ]
     prep = [
         fetch(gain, s.gain),
@@ -122,18 +122,18 @@
         fetch(atok.at[pl.ds(mine, W)], s.tokidx.at[h]),
         fetch(coords.at[:, pl.ds(mine, W)], s.cpos.at[h]),
         fetch(noise.at[:, pl.ds(mine, W)], s.npos.at[h]),
-        fetch(attnw, s.attn_l),
+        fetch(attnw, s.attnT.at[:, :, pl.ds(0, HALF), :]),
         fetch(outw, s.out_l),
         fetch(pbias.at[:, pl.ds(mine, W)], s.bias_l),
     ]
 
-    sig = jnp.full((1, 128), sigma[0], F32)
+    lane = lax.broadcasted_iota(jnp.int32, (1, 128), 1)
+
+    for c in small:
+        c.wait()
+    sig = jnp.broadcast_to(s.sig[...], (1, 128))
     inv = 1.0 / (1.0 + sig * sig)
     root = jnp.sqrt(inv)
-    lane = lax.broadcasted_iota(jnp.int32, (1, 128), 1)
-
-    for c in small:
-        c.wait()
     counts = s.wc[...].astype(F32)
     win_id = (y * nx + x) * nz + z
     win_lane = lax.broadcasted_iota(jnp.int32, counts.shape, 1)
@@ -188,7 +188,7 @@
     x_tok = give(atok.at[pl.ds(theirs, W)], s.tokidx.at[h])
     x_c = give(coords.at[:, pl.ds(theirs, W)], s.cpos.at[h])
     x_n = give(noise.at[:, pl.ds(theirs, W)], s.npos.at[h])
-    x_attn = give(attnw, s.attn_r)
+    x_attn = give(attnw, s.attnT.at[:, :, pl.ds(HALF, HALF), :])
     x_out = give(outw, s.out_r)
     x_bias = give(pbias.at[:, pl.ds(theirs, W)], s.bias_r)
 
@@ -274,11 +274,7 @@
     x_attn.wait()
     x_out.wait()
     for b in range(BLOCKS):
-        for j in range(4):
-            both = jnp.concatenate(
-                [s.attn_l[b, j].astype(F32), s.attn_r[b, j].astype(F32)], axis=1
-            )
-            s.attnT[b, j * C : (j + 1) * C, :] = turned(both, 0.5 if j == 3 else None)
+        s.attnT[b, 3] = (s.attnT[b, 3].astype(F32) * 0.5).astype(BF16)
         both = jnp.concatenate([s.out_l[b].astype(F32), s.out_r[b].astype(F32)], axis=0)
         s.outT[b] = turned(both, 0.25)
     x_bias.wait()
@@ -303,7 +299,7 @@
     s.shift[...] = shift
 
     q_scale = LOG2E * HEAD_DIM ** (-0.5)
-    pairs = GROUP // 2
+    quads = NP // 2
 
     def begin(p, carry):
         for w in range(2):
@@ -313,78 +309,133 @@
 
     lax.fori_loop(0, NP, begin, 0)
 
-    def block(step, carry):
-        b = lax.rem(step, BLOCKS)
-        base = (step // BLOCKS) * pairs
-
-        def term(i, j, w):
-            return s.ada[base + i, b * 6 + j, :, pl.ds(w * QW, QW)]
-
-        for i in range(pairs):
+    def halves(w):
+        return slice(w * QW, (w + 1) * QW)
+
+    def project(b, quad, par):
+        def normed(i, w):
+            p, lanes = 2 * quad + i, halves(w)
+            centred, rstd = norm(s.stream[p, :, lanes])
+            n = centred * (0.5 * rstd) * s.ada[p, b * 6, :, lanes] + s.ada[p, b * 6 + 1, :, lanes]
+            s.n[i, :, lanes] = n.astype(BF16)
+
+        def proj(i):
+            y = mm(s.attnT[b].reshape(4 * C, C), s.n[i])
+            s.q[par, i] = (y[:C] * q_scale).astype(BF16)
             for w in range(2):
-                lanes = pl.ds(w * QW, QW)
-                centred, rstd = norm(s.stream[base + i, :, lanes])
-                n = centred * (0.5 * rstd) * term(i, 0, w) + term(i, 1, w)
-                s.n[i, :, lanes] = n.astype(BF16)
-        for i in range(pairs):
-            proj = mm(s.attnT[b], s.n[i])
-            s.q[i] = (proj[:C] * q_scale).astype(BF16)
-            s.v[i] = proj[2 * C : 3 * C].astype(BF16)
-            s.gate[i] = 1.0 + jnp.tanh(proj[3 * C :])
+                s.k[par, 2 * i + w] = y[C : 2 * C, halves(w)].T.astype(BF16)
+            s.v[par, i] = y[2 * C : 3 * C].astype(BF16)
+            s.gate[par, i] = 1.0 + jnp.tanh(y[3 * C :])
+
+        return [
+            functools.partial(normed, 0, 0),
+            functools.partial(normed, 0, 1),
+            functools.partial(proj, 0),
+            functools.partial(normed, 1, 0),
+            functools.partial(normed, 1, 1),
+            functools.partial(proj, 1),
+        ]
+
+    def attend(b, quad, par):
+        held = {}
+
+        def scores(i, w, hp):
+            cols = []
+            for a in range(2):
+                at = (2 * hp + a) * HEAD_DIM
+                part = [s.q[par, i, at : at + HEAD_DIM, halves(w)]]
+                if at > 0:
+                    part = [jnp.zeros((at, QW), BF16)] + part
+                if at + HEAD_DIM < C:
+                    part = part + [jnp.zeros((C - HEAD_DIM - at, QW), BF16)]
+                cols.append(jnp.concatenate(part, axis=0))
+            held[i, w, hp] = mm(s.k[par, 2 * i + w], jnp.concatenate(cols, axis=1))
+
+        def mix(i, w, hp):
+            both = held.pop((i, w, hp))
+            for a in range(2):
+                hd = 2 * hp + a
+                at = slice(hd * HEAD_DIM, (hd + 1) * HEAD_DIM)
+                sc = both[:, halves(a)] + s.biasT[4 * quad + 2 * i + w, :, halves(hd)]
+                e = jnp.exp2(sc - jnp.max(sc, axis=0, keepdims=True))
+                recip = 1.0 / jnp.sum(e, axis=0, keepdims=True)
+                o = mm(s.v[par, i, at, halves(w)], e.astype(BF16))
+                s.att[par, i, at, halves(w)] = (
+                    o * recip * s.gate[par, i, at, halves(w)]
+                ).astype(BF16)
+
+        units = [(i, w, hp) for i in range(2) for w in range(2) for hp in range(2)]
+        out = [functools.partial(scores, *units[0])]
+        for n, unit in enumerate(units):
+            if n + 1 < len(units):
+                out.append(functools.partial(scores, *units[n + 1]))
+            out.append(functools.partial(mix, *unit))
+        return out
+
+    def add_attended(b, quad, par):
+        def piece(i):
+            p = 2 * quad + i
+            update = mm(s.outT[b], s.att[par, i])
             for w in range(2):
-                s.k[2 * i + w] = proj[C : 2 * C, w * QW : (w + 1) * QW].T.astype(BF16)
-        for i in range(pairs):
-            for w in range(2):
-                lanes = pl.ds(w * QW, QW)
-                keys = s.k[2 * i + w]
-                attended = []
-                for hp in range(2):
-                    cols = []
-                    for a in range(2):
-                        at = (2 * hp + a) * HEAD_DIM
-                        part = [s.q[i, at : at + HEAD_DIM, lanes]]
-                        if at > 0:
-                            part = [jnp.zeros((at, QW), BF16)] + part
-                        if at + HEAD_DIM < C:
-                            part = part + [jnp.zeros((C - HEAD_DIM - at, QW), BF16)]
-                        cols.append(jnp.concatenate(part, axis=0))
-                    scores = mm(keys, jnp.concatenate(cols, axis=1))
-                    for a in range(2):
-                        hd = 2 * hp + a
-                        sc = (
-                            scores[:, a * QW : (a + 1) * QW]
-                            + s.biasT[2 * (base + i) + w, :, hd * QW : (hd + 1) * QW]
-                        )
-                        e = jnp.exp2(sc - jnp.max(sc, axis=0, keepdims=True))
-                        recip = 1.0 / jnp.sum(e, axis=0, keepdims=True)
-                        at = hd * HEAD_DIM
-                        o = mm(s.v[i, at : at + HEAD_DIM, lanes], e.astype(BF16))
-                        attended.append(o * recip)
-                both = jnp.concatenate(attended, axis=0) * s.gate[i, :, lanes]
-                s.att[i, :, lanes] = both.astype(BF16)
-        for i in range(pairs):
-            update = mm(s.outT[b], s.att[i])
-            for w in range(2):
-                lanes = pl.ds(w * QW, QW)
-                xs = s.stream[base + i, :, lanes] + term(i, 2, w) * update[:, w * QW : (w + 1) * QW]
-                s.stream[base + i, :, lanes] = xs
+                lanes = halves(w)
+                xs = s.stream[p, :, lanes] + s.ada[p, b * 6 + 2, :, lanes] * update[:, lanes]
+                s.mid[par, i, :, lanes] = xs
                 centred, rstd = norm(xs)
-                n = centred * (0.5 * rstd) * term(i, 3, w) + term(i, 4, w)
-                s.n[i, :, lanes] = n.astype(BF16)
-        for i in range(pairs):
-            both = mm(s.guT[b], s.n[i])
+                n = centred * (0.5 * rstd) * s.ada[p, b * 6 + 3, :, lanes]
+                s.n2[par, i, :, lanes] = (n + s.ada[p, b * 6 + 4, :, lanes]).astype(BF16)
+
+        return [functools.partial(piece, i) for i in range(2)]
+
+    def transition(b, quad, par):
+        def up(i):
+            both = mm(s.guT[b], s.n2[par, i])
             g = both[:HID]
             s.hidden[i] = (g * (1.0 + jnp.tanh(g)) * both[HID:]).astype(BF16)
-        for i in range(pairs):
-            down = mm(s.downT[b], s.hidden[i])
+
+        def down(i):
+            p = 2 * quad + i
+            d = mm(s.downT[b], s.hidden[i])
             for w in range(2):
-                lanes = pl.ds(w * QW, QW)
-                s.stream[base + i, :, lanes] = (
-                    s.stream[base + i, :, lanes] + term(i, 5, w) * down[:, w * QW : (w + 1) * QW]
+                lanes = halves(w)
+                s.stream[p, :, lanes] = (
+                    s.mid[par, i, :, lanes] + s.ada[p, b * 6 + 5, :, lanes] * d[:, lanes]
                 )
+
+        return [
+            functools.partial(up, 0),
+            functools.partial(up, 1),
+            functools.partial(down, 0),
+            functools.partial(down, 1),
+        ]
+
+    steps = (project, attend, add_attended, transition)
+
+    def slot_of(b, t, first_step, last_step):
+        work = []
+        for n in range(first_step, last_step + 1):
+            quad = (t - n) % quads
+            block_of = b - (n - t + quads - 1) // quads if n > t else b
+            parity = (t - n) % 2
+            pieces = steps[n](block_of, quad, parity if n == 0 else parity)
+            work.append((n, pieces))
+        order = []
+        for n, pieces in work:
+            for at, piece in enumerate(pieces):
+                order.append(((at + 0.5) / len(pieces), -n, piece))
+        for _, _, piece in sorted(order, key=lambda entry: entry[:2]):
+            piece()
+
+    for t in range(quads):
+        slot_of(0, t, 0, min(t, 3))
+
+    def middle(b, carry):
+        for t in range(quads):
+            slot_of(b, t, 0, 3)
         return carry
 
-    lax.fori_loop(0, BLOCKS * (NP // pairs), block, 0)
+    lax.fori_loop(1, BLOCKS, middle, 0)
+    for t in range(3):
+        slot_of(BLOCKS, t, t + 1, 3)
 
     final = jnp.concatenate([s.fin[...].astype(F32), jnp.zeros((5, C), F32)], axis=0).astype(BF16)
 
@@ -427,12 +478,12 @@
     win_total = nz * nxy
     W = slots // 2
     NP = W // 2
-    G = GROUP // 2
     V = pltpu.VMEM
     return {
         "cfull": V((3, slots, HALF), F32),
         "nfull": V((3, slots, HALF), F32),
         "wc": V((1, win_total), jnp.int32),
+        "sig": V((1, 1), F32),
         "gain": V((1, C), F32),
         "pw": V((3, C), F32),
         "adab": V((BLOCKS, 6, C), F32),
@@ -446,8 +497,6 @@
         "tokidx": V((2, W, HALF), jnp.int32),
         "cpos": V((2, 3, W, HALF), F32),
         "npos": V((2, 3, W, HALF), F32),
-        "attn_l": V((BLOCKS, 4, C, HALF), BF16),
-        "attn_r": V((BLOCKS, 4, C, HALF), BF16),
         "out_l": V((BLOCKS, HALF, C), BF16),
         "out_r": V((BLOCKS, HALF, C), BF16),
         "bias_l": V((2, W, QW, QW), BF16),
@@ -459,7 +508,7 @@
         "pwT": V((3, C, C), F32),
         "adabT": V((BLOCKS * 6, C, C), F32),
         "adaT": V((BLOCKS, 6 * C, C), BF16),
-        "attnT": V((BLOCKS, 4 * C, C), BF16),
+        "attnT": V((BLOCKS, 4, C, C), BF16),
         "outT": V((BLOCKS, C, C), BF16),
         "guT": V((BLOCKS, 2 * HID, C), BF16),
         "downT": V((BLOCKS, C, HID), BF16),
@@ -471,13 +520,15 @@
         "ada": V((NP, BLOCKS * 6, C, 2 * QW), F32),
         "biasT": V((W, QW, HEADS * QW), F32),
         "shift": V((C, C), F32),
-        "n": V((G, C, 2 * QW), BF16),
-        "q": V((G, C, 2 * QW), BF16),
-        "k": V((2 * G, QW, C), BF16),
-        "v": V((G, C, 2 * QW), BF16),
-        "gate": V((G, C, 2 * QW), F32),
-        "att": V((G, C, 2 * QW), BF16),
-        "hidden": V((G, HID, 2 * QW), BF16),
+        "n": V((2, C, 2 * QW), BF16),
+        "q": V((2, 2, C, 2 * QW), BF16),
+        "k": V((2, 4, QW, C), BF16),
+        "v": V((2, 2, C, 2 * QW), BF16),
+        "gate": V((2, 2, C, 2 * QW), F32),
+        "att": V((2, 2, C, 2 * QW), BF16),
+        "mid": V((2, 2, C, 2 * QW), F32),
+        "n2": V((2, 2, C, 2 * QW), BF16),
+        "hidden": V((2, HID, 2 * QW), BF16),
         "upd": V((3, W, QW), F32),
         "updr": V((3, W, QW), F32),
         "lsem": pltpu.SemaphoreType.DMA((20,)),
@@ -526,7 +577,7 @@
         return pl.pallas_call(
             body,
             out_shape=jax.ShapeDtypeStruct(coords.shape, F32),
-            in_specs=[pl.BlockSpec(memory_space=pltpu.SMEM)] + [any_spec] * 17,
+            in_specs=[any_spec] * 18,
             out_specs=pl.BlockSpec(memory_space=pltpu.VMEM),
             scratch_shapes=[scratch[name] for name in names],
             compiler_params=pltpu.CompilerParams(
@@ -534,7 +585,7 @@
             ),
             name="denoise",
         )(
-            sigma,
+            sigma.reshape(1, 1),
             coords,
             noise,
             atom_single,
@@ -547,7 +598,7 @@
             position_weight,
             ada_weight,
             ada_bias,
-            attn_weight,
+            jnp.swapaxes(attn_weight, 2, 3),
             out_weight,
             gateup_weight,
             down_weight,

time: 54.9 us -> 41.6 us (0.76)
  Pallas kernels: 50.8 us -> 39.3 us
  local copies, waits for them, and re-layouts: 3.26 us -> 1.42 us
    pallas_call x1, Pallas kernels: 50.8 us -> 39.3 us  [local(): pl.pallas_call(body, out_shape=jax.ShapeDtypeStruct(coords.shape, F32), i...]
    unnamed x2 -> x1, local copies, waits for them, and re-layouts: 3.26 us -> 1.42 us
where the time goes in v2:
time: 41.6 us; the launch traced here: 41.4 us
  Pallas kernels  39.3 us (94%)
  local copies, waits for them, and re-layouts  1.42 us (3%)
  between operations  0.66 us (2%)
    pallas_call x1, Pallas kernels, local(): pl.pallas_call(body, out_shape=jax.ShapeDtypeStruct(coords.shape, F32), i...  39.3 us
    unnamed x1, local copies, waits for them, and re-layouts  1.42 us

profile of v2, /device:TPU:1, one launch (start us, length us, event | category | flops | bytes accessed | tf_op | source)
XLA Modules:
  0.0 41.4 jit_solution(6009946243669582752)
XLA Ops:
  0.7 39.3 %denoise.1 = f32[3,32,64]{2,1,0:T(8,128)} custom-call(f32[1,1]{1,0:T(1,128)} %bitcast.4.refs_0_, f32[3,32,64]{2,1,0:T(8,128)} %refs_1_.1, f32[3,32,64]{2,1,0:T(8,128)} %refs_2_.1, bf16[32,64,128]{2,1,0:T(8,128)(2,1)} %refs_3_.1, bf16[512,384]{1,0:T(8,128)(2,1)} %refs_4_.1, s32[32,64]{1,0:T(8,128)} %refs_5_.1, s32[1,128]{1,0:T(1,128)} %bitcast.6, ...), custom_call_target="tpu_custom_call" | custom-call | tf_op jit(solution)/shard_map/denoise/pallas_call | solution.py:577
  40.0 1.4 %copy.21 = f32[3,32,64]{2,1,0:T(8,128)} copy(f32[3,32,64]{2,1,0:T(8,128)} %denoise.1) | data formatting | bytes 49152

commit v3 on v2

--- a/solution.py
+++ b/solution.py
@@ -72,24 +72,16 @@
     mine = pl.multiple_of(h * W, W)
     theirs = pl.multiple_of(other * W, W)
 
-    n1, n2 = 2 * nz, ny * nx
     me1, me2 = z * 2 + h, y * nx + x
 
-    def dev1(i):
-        return {"win_2": i // 2, "head": lax.rem(i, 2)}
-
-    def dev2(i):
-        return {"win_0": i // nx, "win_1": lax.rem(i, nx)}
-
-    barrier = pltpu.get_barrier_semaphore()
-    for n, me, dev in ((n1, me1, dev1), (n2, me2, dev2)):
-        for j in range(1, n):
-            pl.semaphore_signal(
-                barrier,
-                inc=1,
-                device_id=dev(lax.rem(me + j, n)),
-                device_id_type=pl.DeviceIdType.MESH,
-            )
+    def wrapped(v, n):
+        return jnp.where(v >= n, v - n, v)
+
+    zs = [wrapped(z + d, nz) if d else z for d in range(nz)]
+    ys = [wrapped(y + d, ny) if d else y for d in range(ny)]
+    xs = [wrapped(x + d, nx) if d else x for d in range(nx)]
+    peers1 = [({"win_2": c, "head": a}, c * 2 + a) for c in zs for a in (h, other)][1:]
+    peers2 = [({"win_0": c, "win_1": a}, c * nx + a) for c in ys for a in xs][1:]
 
     count = [0]
 
@@ -106,9 +98,9 @@
         fetch(sigma, s.sig),
     ]
     prep = [
-        fetch(gain, s.gain),
-        fetch(posw, s.pw),
-        fetch(adab, s.adab),
+        fetch(gain, s.rows.at[pl.ds(0, 1)]),
+        fetch(posw, s.rows.at[pl.ds(8, 3)]),
+        *[fetch(adab.at[b], s.rows.at[pl.ds(16 + 8 * b, 6)]) for b in range(BLOCKS)],
         fetch(finw, s.fin),
         fetch(tokw, s.tokw),
         fetch(tokens.at[pl.ds(pl.multiple_of(h * W * TOKW, W * TOKW), W * TOKW)], s.tok),
@@ -126,6 +118,12 @@
         fetch(outw, s.out_l),
         fetch(pbias.at[:, pl.ds(mine, W)], s.bias_l),
     ]
+
+    barrier = pltpu.get_barrier_semaphore()
+    for dev, _ in peers1 + peers2:
+        pl.semaphore_signal(
+            barrier, inc=1, device_id=dev, device_id_type=pl.DeviceIdType.MESH
+        )
 
     lane = lax.broadcasted_iota(jnp.int32, (1, 128), 1)
 
@@ -148,7 +146,7 @@
         row = jnp.where(lane == k, part, row)
     s.red1[me1] = row
 
-    pl.semaphore_wait(barrier, n1 - 1 + n2 - 1)
+    pl.semaphore_wait(barrier, len(peers1) + len(peers2))
 
     def remote(src, dst, send, recv, dev):
         return pltpu.make_async_remote_copy(
@@ -160,20 +158,19 @@
             device_id_type=pl.DeviceIdType.MESH,
         )
 
-    def spread(buf, n, me, dev, ssem, rsem):
+    def spread(buf, me, peers, ssem, rsem):
         sends = []
-        for j in range(1, n):
-            c = remote(buf.at[me], buf.at[me], ssem.at[j], rsem.at[me], dev(lax.rem(me + j, n)))
+        for j, (dev, _) in enumerate(peers):
+            c = remote(buf.at[me], buf.at[me], ssem.at[j], rsem.at[me], dev)
             c.start()
             sends.append(c)
         return sends
 
-    def collect(buf, n, me, dev, ssem, rsem):
-        for j in range(1, n):
-            src = lax.rem(me + j, n)
-            remote(buf.at[src], buf.at[src], ssem.at[j], rsem.at[src], dev(src)).wait_recv()
-
-    sends1 = spread(s.red1, n1, me1, dev1, s.ssem1, s.rsem1)
+    def collect(buf, peers, ssem, rsem):
+        for j, (dev, src) in enumerate(peers):
+            remote(buf.at[src], buf.at[src], ssem.at[j], rsem.at[src], dev).wait_recv()
+
+    sends1 = spread(s.red1, me1, peers1, s.ssem1, s.rsem1)
 
     pair = [0]
 
@@ -193,20 +190,25 @@
     x_bias = give(pbias.at[:, pl.ds(theirs, W)], s.bias_r)
 
     def turned(values, scale=None):
-        values = values.astype(F32)
+        values = values.T
         if scale is not None:
-            values = values * scale
-        return values.T.astype(BF16)
+            values = values * jnp.asarray(scale, BF16)
+        return values
 
     for c in prep:
         c.wait()
     s.tokwT[...] = turned(s.tokw[...])
-    s.gainT[...] = jnp.broadcast_to(s.gain[...], (C, C)).T
+    columns = s.rows[...].T
+
+    def column(k):
+        return jnp.broadcast_to(columns[:, k : k + 1], (C, C))
+
+    s.gainT[...] = column(0)
     for k in range(3):
-        s.pwT[k] = jnp.broadcast_to(s.pw[k : k + 1, :], (C, C)).T
+        s.pwT[k] = column(8 + k)
     for b in range(BLOCKS):
         for j in range(6):
-            bias = jnp.broadcast_to(s.adab[b][j : j + 1, :], (C, C)).T
+            bias = column(16 + 8 * b + j)
             s.adabT[b * 6 + j] = bias * 0.5 if j in (0, 2, 3, 5) else bias
     c_ada.wait()
     for b in range(BLOCKS):
@@ -235,7 +237,7 @@
         lax.broadcasted_iota(jnp.int32, (C, C), 0) == lax.broadcasted_iota(jnp.int32, (C, C), 1)
     ).astype(BF16)
 
-    def condition(p):
+    def condition(p, at):
         for w in range(2):
             lanes = pl.ds(w * QW, QW)
             win = 2 * p + w
@@ -244,51 +246,58 @@
             one_hot = jnp.where(ids == own, 1.0, 0.0).astype(BF16)
             cond = mm(eye, s.atoms[win], NT) + mm(s.tpT[...], one_hot)
             centred, rstd = norm(cond)
-            s.cn[:, lanes] = (centred * rstd * s.gainT[...]).astype(BF16)
+            s.cn[at, :, lanes] = (centred * rstd * s.gainT[...]).astype(BF16)
             for k in range(3):
                 cond = cond + s.pos[k, pl.ds(win, 1), :] * s.pwT[k]
             s.stream[p, :, lanes] = cond
+
+    def ada_terms(p, at, b):
+        terms = mm(s.adaT[b], s.cn[at])
+        for j in range(6):
+            for w in range(2):
+                lanes = pl.ds(w * QW, QW)
+                a = terms[j * C : (j + 1) * C, w * QW : (w + 1) * QW] + s.adabT[b * 6 + j]
+                if j in (0, 2, 3, 5):
+                    a = 1.0 + jnp.tanh(a)
+                s.ada[p, b * 6 + j, :, lanes] = a
+
+    def first(step, carry):
+        condition(2 * step, 0)
+        condition(2 * step + 1, 1)
         for b in range(BLOCKS):
-            terms = mm(s.adaT[b], s.cn[...])
-            for j in range(6):
-                for w in range(2):
-                    lanes = pl.ds(w * QW, QW)
-                    a = terms[j * C : (j + 1) * C, w * QW : (w + 1) * QW] + s.adabT[b * 6 + j]
-                    if j in (0, 2, 3, 5):
-                        a = 1.0 + jnp.tanh(a)
-                    s.ada[p, b * 6 + j, :, lanes] = a
-
-    def first(p, carry):
-        condition(p)
+            for at in range(2):
+                ada_terms(2 * step + at, at, b)
         return carry
 
-    half = NP // 2
+    half = NP // 4
     lax.fori_loop(0, half, first, 0)
 
-    collect(s.red1, n1, me1, dev1, s.ssem1, s.rsem1)
+    collect(s.red1, peers1, s.ssem1, s.rsem1)
     s.red2[me2] = jnp.sum(s.red1[...], axis=0)
-    sends2 = spread(s.red2, n2, me2, dev2, s.ssem2, s.rsem2)
-
-    lax.fori_loop(half, NP, first, 0)
+    sends2 = spread(s.red2, me2, peers2, s.ssem2, s.rsem2)
+
+    lax.fori_loop(half, NP // 2, first, 0)
 
     x_attn.wait()
     x_out.wait()
     for b in range(BLOCKS):
         s.attnT[b, 3] = (s.attnT[b, 3].astype(F32) * 0.5).astype(BF16)
-        both = jnp.concatenate([s.out_l[b].astype(F32), s.out_r[b].astype(F32)], axis=0)
+        both = jnp.concatenate([s.out_l[b], s.out_r[b]], axis=0)
         s.outT[b] = turned(both, 0.25)
     x_bias.wait()
 
-    def turn_bias(w, carry):
-        for a in range(HALF_HEADS):
-            for side, buf in enumerate((s.bias_l, s.bias_r)):
-                i = side * HALF_HEADS + a
-                s.biasT[w, :, i * QW : (i + 1) * QW] = (buf[a, w].astype(F32) * LOG2E).T
+    def turn_bias(step, carry):
+        for n in range(4):
+            w = 4 * step + n
+            for a in range(HALF_HEADS):
+                for side, buf in enumerate((s.bias_l, s.bias_r)):
+                    i = side * HALF_HEADS + a
+                    s.biasT[w, :, i * QW : (i + 1) * QW] = buf[a, w].T.astype(F32) * LOG2E
         return carry
 
-    lax.fori_loop(0, W, turn_bias, 0)
-
-    collect(s.red2, n2, me2, dev2, s.ssem2, s.rsem2)
+    lax.fori_loop(0, W // 4, turn_bias, 0)
+
+    collect(s.red2, peers2, s.ssem2, s.rsem2)
     total = jnp.sum(s.red2[...], axis=0) / atoms_total
     centre = [
         jnp.sum(jnp.where(lane == k, total, 0.0), axis=1, keepdims=True) for k in range(3)
@@ -312,100 +321,100 @@
     def halves(w):
         return slice(w * QW, (w + 1) * QW)
 
+    def place(quad, v):
+        return 2 * quad + v // 2, halves(v % 2)
+
     def project(b, quad, par):
-        def normed(i, w):
-            p, lanes = 2 * quad + i, halves(w)
+        def normed(v):
+            p, lanes = place(quad, v)
             centred, rstd = norm(s.stream[p, :, lanes])
             n = centred * (0.5 * rstd) * s.ada[p, b * 6, :, lanes] + s.ada[p, b * 6 + 1, :, lanes]
-            s.n[i, :, lanes] = n.astype(BF16)
-
-        def proj(i):
-            y = mm(s.attnT[b].reshape(4 * C, C), s.n[i])
-            s.q[par, i] = (y[:C] * q_scale).astype(BF16)
-            for w in range(2):
-                s.k[par, 2 * i + w] = y[C : 2 * C, halves(w)].T.astype(BF16)
-            s.v[par, i] = y[2 * C : 3 * C].astype(BF16)
-            s.gate[par, i] = 1.0 + jnp.tanh(y[3 * C :])
-
-        return [
-            functools.partial(normed, 0, 0),
-            functools.partial(normed, 0, 1),
-            functools.partial(proj, 0),
-            functools.partial(normed, 1, 0),
-            functools.partial(normed, 1, 1),
-            functools.partial(proj, 1),
+            s.n[:, halves(v)] = n.astype(BF16)
+
+        def proj(j0):
+          yy = mm(s.attnT[b, j0 : j0 + 2].reshape(2 * C, C), s.n[...])
+          for j in (j0, j0 + 1):
+            y = yy[(j - j0) * C : (j - j0 + 1) * C]
+            if j == 0:
+                s.q[par] = (y * q_scale).astype(BF16)
+            elif j == 1:
+                for v in range(4):
+                    s.k[par, v] = y[:, halves(v)].T.astype(BF16)
+            elif j == 2:
+                s.v[par] = y.astype(BF16)
+            else:
+                s.gate[par] = 1.0 + jnp.tanh(y)
+
+        return [functools.partial(normed, v) for v in range(4)] + [
+            functools.partial(proj, j) for j in (0, 2)
         ]
 
     def attend(b, quad, par):
         held = {}
 
-        def scores(i, w, hp):
+        def scores(v):
             cols = []
-            for a in range(2):
-                at = (2 * hp + a) * HEAD_DIM
-                part = [s.q[par, i, at : at + HEAD_DIM, halves(w)]]
+            for hd in range(HEADS):
+                at = hd * HEAD_DIM
+                part = [s.q[par, at : at + HEAD_DIM, halves(v)]]
                 if at > 0:
                     part = [jnp.zeros((at, QW), BF16)] + part
                 if at + HEAD_DIM < C:
                     part = part + [jnp.zeros((C - HEAD_DIM - at, QW), BF16)]
                 cols.append(jnp.concatenate(part, axis=0))
-            held[i, w, hp] = mm(s.k[par, 2 * i + w], jnp.concatenate(cols, axis=1))
-
-        def mix(i, w, hp):
-            both = held.pop((i, w, hp))
-            for a in range(2):
-                hd = 2 * hp + a
-                at = slice(hd * HEAD_DIM, (hd + 1) * HEAD_DIM)
-                sc = both[:, halves(a)] + s.biasT[4 * quad + 2 * i + w, :, halves(hd)]
-                e = jnp.exp2(sc - jnp.max(sc, axis=0, keepdims=True))
-                recip = 1.0 / jnp.sum(e, axis=0, keepdims=True)
-                o = mm(s.v[par, i, at, halves(w)], e.astype(BF16))
-                s.att[par, i, at, halves(w)] = (
-                    o * recip * s.gate[par, i, at, halves(w)]
-                ).astype(BF16)
-
-        units = [(i, w, hp) for i in range(2) for w in range(2) for hp in range(2)]
-        out = [functools.partial(scores, *units[0])]
-        for n, unit in enumerate(units):
-            if n + 1 < len(units):
-                out.append(functools.partial(scores, *units[n + 1]))
-            out.append(functools.partial(mix, *unit))
+            held[v] = mm(s.k[par, v], jnp.concatenate(cols, axis=1))
+
+        def mix(v, hd):
+            at = slice(hd * HEAD_DIM, (hd + 1) * HEAD_DIM)
+            sc = held[v][:, halves(hd)] + s.biasT[4 * quad + v, :, halves(hd)]
+            e = jnp.exp2(sc - jnp.max(sc, axis=0, keepdims=True))
+            recip = 1.0 / jnp.sum(e, axis=0, keepdims=True)
+            o = mm(s.v[par, at, halves(v)], e.astype(BF16))
+            s.att[par, at, halves(v)] = (o * recip * s.gate[par, at, halves(v)]).astype(BF16)
+
+        out = [functools.partial(scores, 0)]
+        for v in range(4):
+            if v + 1 < 4:
+                out.append(functools.partial(scores, v + 1))
+            out += [functools.partial(mix, v, hd) for hd in range(HEADS)]
         return out
 
     def add_attended(b, quad, par):
-        def piece(i):
-            p = 2 * quad + i
-            update = mm(s.outT[b], s.att[par, i])
-            for w in range(2):
-                lanes = halves(w)
-                xs = s.stream[p, :, lanes] + s.ada[p, b * 6 + 2, :, lanes] * update[:, lanes]
-                s.mid[par, i, :, lanes] = xs
-                centred, rstd = norm(xs)
-                n = centred * (0.5 * rstd) * s.ada[p, b * 6 + 3, :, lanes]
-                s.n2[par, i, :, lanes] = (n + s.ada[p, b * 6 + 4, :, lanes]).astype(BF16)
-
-        return [functools.partial(piece, i) for i in range(2)]
+        held = {}
+
+        def update():
+            held[0] = mm(s.outT[b], s.att[par])
+
+        def piece(v):
+            p, lanes = place(quad, v)
+            xs = s.stream[p, :, lanes] + s.ada[p, b * 6 + 2, :, lanes] * held[0][:, halves(v)]
+            s.mid[par, :, halves(v)] = xs
+            centred, rstd = norm(xs)
+            n = centred * (0.5 * rstd) * s.ada[p, b * 6 + 3, :, lanes]
+            s.n2[par, :, halves(v)] = (n + s.ada[p, b * 6 + 4, :, lanes]).astype(BF16)
+
+        return [update] + [functools.partial(piece, v) for v in range(4)]
 
     def transition(b, quad, par):
-        def up(i):
-            both = mm(s.guT[b], s.n2[par, i])
-            g = both[:HID]
-            s.hidden[i] = (g * (1.0 + jnp.tanh(g)) * both[HID:]).astype(BF16)
-
-        def down(i):
-            p = 2 * quad + i
-            d = mm(s.downT[b], s.hidden[i])
-            for w in range(2):
-                lanes = halves(w)
-                s.stream[p, :, lanes] = (
-                    s.mid[par, i, :, lanes] + s.ada[p, b * 6 + 5, :, lanes] * d[:, lanes]
-                )
-
-        return [
-            functools.partial(up, 0),
-            functools.partial(up, 1),
-            functools.partial(down, 0),
-            functools.partial(down, 1),
+        held = {}
+
+        def up(j):
+            rows = slice(j * C, (j + 1) * C)
+            g = mm(s.guT[b, rows, :], s.n2[par])
+            u = mm(s.guT[b, HID + j * C : HID + (j + 1) * C, :], s.n2[par])
+            s.hidden[rows, :] = (g * (1.0 + jnp.tanh(g)) * u).astype(BF16)
+
+        def down():
+            held[0] = mm(s.downT[b], s.hidden[...])
+
+        def piece(v):
+            p, lanes = place(quad, v)
+            s.stream[p, :, lanes] = (
+                s.mid[par, :, halves(v)] + s.ada[p, b * 6 + 5, :, lanes] * held[0][:, halves(v)]
+            )
+
+        return [functools.partial(up, 0), functools.partial(up, 1), down] + [
+            functools.partial(piece, v) for v in range(4)
         ]
 
     steps = (project, attend, add_attended, transition)
@@ -484,9 +493,7 @@
         "nfull": V((3, slots, HALF), F32),
         "wc": V((1, win_total), jnp.int32),
         "sig": V((1, 1), F32),
-        "gain": V((1, C), F32),
-        "pw": V((3, C), F32),
-        "adab": V((BLOCKS, 6, C), F32),
+        "rows": V((C, C), F32),
         "fin": V((3, C), BF16),
         "tokw": V((3 * C, C), BF16),
         "tok": V((W * TOKW, 3 * C), BF16),
@@ -515,23 +522,23 @@
         "tpT": V((C, W * TOKW), BF16),
         "tokcat": V((W, QW), jnp.int32),
         "pos": V((3, W, QW), F32),
-        "cn": V((C, 2 * QW), BF16),
+        "cn": V((2, C, 2 * QW), BF16),
         "stream": V((NP, C, 2 * QW), F32),
         "ada": V((NP, BLOCKS * 6, C, 2 * QW), F32),
         "biasT": V((W, QW, HEADS * QW), F32),
         "shift": V((C, C), F32),
-        "n": V((2, C, 2 * QW), BF16),
-        "q": V((2, 2, C, 2 * QW), BF16),
+        "n": V((C, 4 * QW), BF16),
+        "q": V((2, C, 4 * QW), BF16),
         "k": V((2, 4, QW, C), BF16),
-        "v": V((2, 2, C, 2 * QW), BF16),
-        "gate": V((2, 2, C, 2 * QW), F32),
-        "att": V((2, 2, C, 2 * QW), BF16),
-        "mid": V((2, 2, C, 2 * QW), F32),
-        "n2": V((2, 2, C, 2 * QW), BF16),
-        "hidden": V((2, HID, 2 * QW), BF16),
+        "v": V((2, C, 4 * QW), BF16),
+        "gate": V((2, C, 4 * QW), F32),
+        "att": V((2, C, 4 * QW), BF16),
+        "mid": V((2, C, 4 * QW), F32),
+        "n2": V((2, C, 4 * QW), BF16),
+        "hidden": V((HID, 4 * QW), BF16),
         "upd": V((3, W, QW), F32),
         "updr": V((3, W, QW), F32),
-        "lsem": pltpu.SemaphoreType.DMA((20,)),
+        "lsem": pltpu.SemaphoreType.DMA((24,)),
         "ssem1": pltpu.SemaphoreType.DMA((2 * nz,)),
         "rsem1": pltpu.SemaphoreType.DMA((2 * nz,)),
         "ssem2": pltpu.SemaphoreType.DMA((nxy,)),

time: 41.6 us -> 38.2 us (0.918)
  Pallas kernels: 39.3 us -> 36 us
    pallas_call x1, Pallas kernels: 39.3 us -> 36 us  [local(): pl.pallas_call(body, out_shape=jax.ShapeDtypeStruct(coords.shape, F32), i...]
where the time goes in v3:
time: 38.2 us; the launch traced here: 38 us
  Pallas kernels  36 us (94%)
  local copies, waits for them, and re-layouts  1.42 us (4%)
  between operations  0.66 us (2%)
    pallas_call x1, Pallas kernels, local(): pl.pallas_call(body, out_shape=jax.ShapeDtypeStruct(coords.shape, F32), i...  36 us
    unnamed x1, local copies, waits for them, and re-layouts  1.42 us

profile of v3, /device:TPU:1, one launch (start us, length us, event | category | flops | bytes accessed | tf_op | source)
XLA Modules:
  0.0 38.0 jit_solution(14980630957266763215)
XLA Ops:
  0.7 36.0 %denoise.1 = f32[3,32,64]{2,1,0:T(8,128)} custom-call(f32[1,1]{1,0:T(1,128)} %bitcast.4.refs_0_, f32[3,32,64]{2,1,0:T(8,128)} %refs_1_.1, f32[3,32,64]{2,1,0:T(8,128)} %refs_2_.1, bf16[32,64,128]{2,1,0:T(8,128)(2,1)} %refs_3_.1, bf16[512,384]{1,0:T(8,128)(2,1)} %refs_4_.1, s32[32,64]{1,0:T(8,128)} %refs_5_.1, s32[1,128]{1,0:T(1,128)} %bitcast.6, ...), custom_call_target="tpu_custom_call" | custom-call | tf_op jit(solution)/shard_map/denoise/pallas_call | solution.py:584
  36.6 1.4 %copy.21 = f32[3,32,64]{2,1,0:T(8,128)} copy(f32[3,32,64]{2,1,0:T(8,128)} %denoise.1) | data formatting | bytes 49152

commit v4 on v3

--- a/solution.py
+++ b/solution.py
@@ -369,35 +369,41 @@
             sc = held[v][:, halves(hd)] + s.biasT[4 * quad + v, :, halves(hd)]
             e = jnp.exp2(sc - jnp.max(sc, axis=0, keepdims=True))
             recip = 1.0 / jnp.sum(e, axis=0, keepdims=True)
-            o = mm(s.v[par, at, halves(v)], e.astype(BF16))
+            held[v, hd] = (mm(s.v[par, at, halves(v)], e.astype(BF16)), recip)
+
+        def close(v, hd):
+            at = slice(hd * HEAD_DIM, (hd + 1) * HEAD_DIM)
+            o, recip = held.pop((v, hd))
             s.att[par, at, halves(v)] = (o * recip * s.gate[par, at, halves(v)]).astype(BF16)
 
-        out = [functools.partial(scores, 0)]
-        for v in range(4):
-            if v + 1 < 4:
-                out.append(functools.partial(scores, v + 1))
-            out += [functools.partial(mix, v, hd) for hd in range(HEADS)]
-        return out
+        units = [(v, hd) for v in range(4) for hd in range(HEADS)]
+        out = [functools.partial(scores, v) for v in range(2)]
+        for n, (v, hd) in enumerate(units):
+            if hd == 0 and v + 2 < 4:
+                out.append(functools.partial(scores, v + 2))
+            out.append(functools.partial(mix, v, hd))
+            if n >= 1:
+                out.append(functools.partial(close, *units[n - 1]))
+        return out + [functools.partial(close, *unit) for unit in units[-1:]]
 
     def add_attended(b, quad, par):
-        held = {}
-
         def update():
-            held[0] = mm(s.outT[b], s.att[par])
+            u = mm(s.outT[b], s.att[par])
+            for v in range(4):
+                p, lanes = place(quad, v)
+                s.mid[par, :, halves(v)] = (
+                    s.stream[p, :, lanes] + s.ada[p, b * 6 + 2, :, lanes] * u[:, halves(v)]
+                )
 
         def piece(v):
             p, lanes = place(quad, v)
-            xs = s.stream[p, :, lanes] + s.ada[p, b * 6 + 2, :, lanes] * held[0][:, halves(v)]
-            s.mid[par, :, halves(v)] = xs
-            centred, rstd = norm(xs)
+            centred, rstd = norm(s.mid[par, :, halves(v)])
             n = centred * (0.5 * rstd) * s.ada[p, b * 6 + 3, :, lanes]
             s.n2[par, :, halves(v)] = (n + s.ada[p, b * 6 + 4, :, lanes]).astype(BF16)
 
         return [update] + [functools.partial(piece, v) for v in range(4)]
 
     def transition(b, quad, par):
-        held = {}
-
         def up(j):
             rows = slice(j * C, (j + 1) * C)
             g = mm(s.guT[b, rows, :], s.n2[par])
@@ -405,17 +411,14 @@
             s.hidden[rows, :] = (g * (1.0 + jnp.tanh(g)) * u).astype(BF16)
 
         def down():
-            held[0] = mm(s.downT[b], s.hidden[...])
-
-        def piece(v):
-            p, lanes = place(quad, v)
-            s.stream[p, :, lanes] = (
-                s.mid[par, :, halves(v)] + s.ada[p, b * 6 + 5, :, lanes] * held[0][:, halves(v)]
-            )
-
-        return [functools.partial(up, 0), functools.partial(up, 1), down] + [
-            functools.partial(piece, v) for v in range(4)
-        ]
+            d = mm(s.downT[b], s.hidden[...])
+            for v in range(4):
+                p, lanes = place(quad, v)
+                s.stream[p, :, lanes] = (
+                    s.mid[par, :, halves(v)] + s.ada[p, b * 6 + 5, :, lanes] * d[:, halves(v)]
+                )
+
+        return [functools.partial(up, 0), functools.partial(up, 1), down]
 
     steps = (project, attend, add_attended, transition)
 
@@ -448,15 +451,16 @@
 
     final = jnp.concatenate([s.fin[...].astype(F32), jnp.zeros((5, C), F32)], axis=0).astype(BF16)
 
-    def finish(p, carry):
-        for w in range(2):
-            centred, rstd = norm(s.stream[p, :, pl.ds(w * QW, QW)])
+    def finish(quad, carry):
+        for v in range(4):
+            p, lanes = place(quad, v)
+            centred, rstd = norm(s.stream[p, :, lanes])
             upd = mm(final, (centred * rstd).astype(BF16))
             for k in range(3):
-                s.upd[k, pl.ds(2 * p + w, 1), :] = upd[k : k + 1, :]
+                s.upd[k, pl.ds(4 * quad + v, 1), :] = upd[k : k + 1, :]
         return carry
 
-    lax.fori_loop(0, NP, finish, 0)
+    lax.fori_loop(0, quads, finish, 0)
     x_upd = give(s.upd, s.updr)
 
     def write(source, first_slot):
@@ -583,12 +587,12 @@
         any_spec = pl.BlockSpec(memory_space=pl.ANY)
         return pl.pallas_call(
             body,
-            out_shape=jax.ShapeDtypeStruct(coords.shape, F32),
+            out_shape=pltpu.VMEM(coords.shape, F32),
             in_specs=[any_spec] * 18,
             out_specs=pl.BlockSpec(memory_space=pltpu.VMEM),
             scratch_shapes=[scratch[name] for name in names],
             compiler_params=pltpu.CompilerParams(
-                collective_id=0, has_side_effects=True, vmem_limit_bytes=60 * 1024 * 1024
+                collective_id=0, has_side_effects=True, vmem_limit_bytes=56 * 1024 * 1024
             ),
             name="denoise",
         )(

time: 38.2 us -> 35.5 us (0.929)
  Pallas kernels: 36 us -> 34.1 us
  local copies, waits for them, and re-layouts: 1.42 us -> 0.62 us
    pallas_call x1, Pallas kernels: 36 us -> 34.1 us  [local(): pl.pallas_call(body, out_shape=pltpu.VMEM(coords.shape, F32), in_specs=[a...]
    unnamed x1, local copies, waits for them, and re-layouts: 1.42 us -> 0.62 us
where the time goes in v4:
time: 35.5 us; the launch traced here: 35.4 us
  Pallas kernels  34.1 us (96%)
  between operations  0.66 us (2%)
  local copies, waits for them, and re-layouts  0.62 us (2%)
    pallas_call x1, Pallas kernels, local(): pl.pallas_call(body, out_shape=pltpu.VMEM(coords.shape, F32), in_specs=[a...  34.1 us

profile of v4, /device:TPU:1, one launch (start us, length us, event | category | flops | bytes accessed | tf_op | source)
XLA Modules:
  0.0 35.4 jit_solution(11814810469064609787)
XLA Ops:
  0.7 34.1 %denoise.1 = f32[3,32,64]{2,1,0:T(8,128)S(1)} custom-call(f32[1,1]{1,0:T(1,128)} %bitcast.4.refs_0_, f32[3,32,64]{2,1,0:T(8,128)} %refs_1_.1, f32[3,32,64]{2,1,0:T(8,128)} %refs_2_.1, bf16[32,64,128]{2,1,0:T(8,128)(2,1)} %refs_3_.1, bf16[512,384]{1,0:T(8,128)(2,1)} %refs_4_.1, s32[32,64]{1,0:T(8,128)} %refs_5_.1, s32[1,128]{1,0:T(1,128)} %bitcast.6, ...), custom_call_target="tpu_custom_call" | custom-call | tf_op jit(solution)/shard_map/denoise/pallas_call | solution.py:588
  34.8 0.6 %copy.20 = f32[3,32,64]{2,1,0:T(8,128)} copy(f32[3,32,64]{2,1,0:T(8,128)S(1)} %denoise.1) | data formatting | bytes 49152
